TPU v7x, 8 devices: a whole 2x2x1 slice. The times are simulated.
8 devices in a mesh: dp: 1 (over z), ep: 8 (over y, x, core).
Axes of the slice: x: 2, y: 2, z: 1, core: 2. Of those that a mesh axis runs over, the one named last changes fastest.
Arguments:
- h0: bfloat16 [8, 256, 2048], P(('dp', 'ep'))
- idx: int32 [8, 256, 8], P(('dp', 'ep'))
- slot: int32 [8, 256, 8], P(('dp', 'ep'))
- norm_attn: bfloat16 [2048], replicated
- wq: bfloat16 [2048, 4096], replicated
- wk: bfloat16 [2048, 512], replicated
- wv: bfloat16 [2048, 512], replicated
- wo: bfloat16 [4096, 2048], replicated
- norm_ffn: bfloat16 [2048], replicated
- w1: bfloat16 [2048, 6144], replicated
- w3: bfloat16 [2048, 6144], replicated
- w2: bfloat16 [6144, 2048], replicated
- norm_moe: bfloat16 [2048], replicated
- wr: bfloat16 [2048, 128], replicated
- ue1: bfloat16 [128, 2048, 768], P('ep')
- ue3: bfloat16 [128, 2048, 768], P('ep')
- ue2: bfloat16 [128, 768, 2048], P('ep')
Outputs:
- output: bfloat16 [8, 256, 2048], P(('dp', 'ep'))
All inputs are finite; a program needn't handle non-finite values.
Results may differ from a plain program's by a relative error of at most 0.0105805.
Values are sent between devices in bfloat16 or wider.
A program may use at most 1 GiB of HBM per device.

v0:
```python
import jax
import jax.numpy as jnp
from jax import lax
from jax.sharding import PartitionSpec as P

HEAD = 128
EPS = 1e-6
ROPE_BASE = 10000.0


def _rms(x, w):
    xf = x.astype(jnp.float32)
    r = lax.rsqrt(jnp.mean(xf * xf, axis=-1, keepdims=True) + EPS)
    return (xf * r * w.astype(jnp.float32)).astype(jnp.bfloat16)


def _rope(x, cos, sin):
    h = HEAD // 2
    x1, x2 = x[..., :h], x[..., h:]
    return jnp.concatenate([x1 * cos - x2 * sin, x2 * cos + x1 * sin], axis=-1)


def _dense(h0, na, wq, wk, wv, wo, nf, w1, w3, w2):
    f32, bf = jnp.float32, jnp.bfloat16
    b, s, d = h0.shape
    nh = wq.shape[1] // HEAD
    nkvv = wk.shape[1] // HEAD
    pos = jnp.arange(s).astype(f32)
    inv = ROPE_BASE ** (-2.0 * jnp.arange(HEAD // 2).astype(f32) / HEAD)
    ang = pos[:, None] * inv[None, :]
    cos, sin = jnp.cos(ang)[:, None, :], jnp.sin(ang)[:, None, :]
    x = _rms(h0, na).reshape(b * s, d)
    q = _rope(jnp.dot(x, wq, preferred_element_type=f32).reshape(b, s, nh, HEAD), cos, sin).astype(bf)
    k = _rope(jnp.dot(x, wk, preferred_element_type=f32).reshape(b, s, nkvv, HEAD), cos, sin).astype(bf)
    v = jnp.dot(x, wv, preferred_element_type=f32).astype(bf).reshape(b, s, nkvv, HEAD)
    q = q.reshape(b, s, nkvv, nh // nkvv, HEAD)
    sc = jnp.einsum('bqgrd,bkgd->bgrqk', q, k, preferred_element_type=f32) * HEAD ** -0.5
    causal = jnp.arange(s)[:, None] >= jnp.arange(s)[None, :]
    sc = jnp.where(causal, sc, -jnp.inf)
    p = jax.nn.softmax(sc, axis=-1).astype(bf)
    o = jnp.einsum('bgrqk,bkgd->bqgrd', p, v, preferred_element_type=f32).astype(bf).reshape(b * s, nh * HEAD)
    a = (h0.reshape(b * s, d).astype(f32) + jnp.dot(o, wo, preferred_element_type=f32)).astype(bf)
    z = _rms(a, nf)
    hid = (jax.nn.silu(jnp.dot(z, w1, preferred_element_type=f32)) * jnp.dot(z, w3, preferred_element_type=f32)).astype(bf)
    return a.astype(f32) + jnp.dot(hid, w2, preferred_element_type=f32)


def _route(h0, nm, wr, idx):
    d = h0.shape[-1]
    k = idx.shape[-1]
    u = _rms(h0, nm).reshape(-1, d)
    logits = jnp.dot(u, wr, preferred_element_type=jnp.float32)
    g = jax.nn.softmax(jnp.take_along_axis(logits, idx.reshape(-1, k), axis=1), axis=-1)
    return u, g


def _experts(x, ue1, ue3, ue2):
    f32 = jnp.float32
    h1 = jnp.einsum('ecd,edf->ecf', x, ue1, preferred_element_type=f32)
    h3 = jnp.einsum('ecd,edf->ecf', x, ue3, preferred_element_type=f32)
    hid = (jax.nn.silu(h1) * h3).astype(jnp.bfloat16)
    return jnp.einsum('ecf,efd->ecd', hid, ue2, preferred_element_type=f32).astype(jnp.bfloat16)


def solution(mesh):
    G = mesh.shape['ep']

    def local(h0, idx, slot, na, wq, wk, wv, wo, nf, w1, w3, w2, nm, wr, ue1, ue3, ue2):
        f32 = jnp.float32
        b, s, d = h0.shape
        t = b * s
        k = idx.shape[-1]
        el = ue1.shape[0]
        e = el * G
        cap = 2 * t * k // e
        u, g = _route(h0, nm, wr, idx)
        ix = idx.reshape(t, k)
        sl = slot.reshape(t, k)
        rows = jnp.broadcast_to(jnp.arange(t, dtype=jnp.int32)[:, None], (t, k))
        tok = jnp.full((e, cap), t, jnp.int32).at[ix, sl].set(rows)
        send = jnp.take(u, tok, axis=0, mode='fill', fill_value=0)
        recv = lax.all_to_all(send, 'ep', 0, 0, tiled=True)
        x = recv.reshape(G, el, cap, d).transpose(1, 0, 2, 3).reshape(el, G * cap, d)
        y = _experts(x, ue1, ue3, ue2)
        y = y.reshape(el, G, cap, d).transpose(1, 0, 2, 3).reshape(e, cap, d)
        back = lax.all_to_all(y, 'ep', 0, 0, tiled=True)
        yg = back[ix, sl]
        m = jnp.sum(g[..., None] * yg.astype(f32), axis=1)
        dense = _dense(h0, na, wq, wk, wv, wo, nf, w1, w3, w2)
        return (dense + m).astype(jnp.bfloat16).reshape(b, s, d)

    rows_spec = P(('dp', 'ep'))
    in_specs = (rows_spec,) * 3 + (P(),) * 11 + (P('ep'),) * 3
    return jax.shard_map(local, mesh=mesh, in_specs=in_specs, out_specs=rows_spec, check_vma=False)
```

profile of v0, /device:TPU:0, one launch (start us, length us, event | category | flops | bytes accessed | tf_op | source)
XLA Modules:
  0.0 605.6 jit_solution(17988446999216059067)
XLA Ops:
  0.0 1.5 shift-left_or_fusion
  1.5 0.7 and_reduce_fusion
  2.2 0.7 multiply_reduce_fusion
  2.9 0.1 copy.50
  3.3 8.1 %scatter_custom_fusion = s32[4096]{0:T(1024)S(1)} fusion(s32[2048]{0:T(1024)S(1)} %reshape.356, s32[2048]{0:T(1024)S(1)} %reshape.358, s32[]{:T(128)} %constant.60.clone.1), kind=kCustom, calls=%fused_computation.86 | custom fusion | bytes 16388
  11.4 1.5 fusion.21
  12.9 0.7 convert_element_type.133
  13.6 0.1 copy.51
  14.0 1.5 fusion.33
  15.5 20.9 %gather_fusion = bf16[4096,2048]{1,0:T(8,128)(2,1)} fusion(bf16[256,2048]{1,0:T(8,128)(2,1)S(1)} %fusion.33, s32[4096]{0:T(1024)S(1)} %broadcast_clamp_fusion), kind=kCustom, calls=%fused_computation | custom fusion | bytes 33570816 | tf_op jit(solution)/shard_map/jit(_take)/gather | solution.py:81
  36.4 8.3 %broadcast_select_fusion = bf16[128,32,2048]{2,1,0:T(8,128)(2,1)S(1)} fusion(bf16[128,32,2048]{2,1,0:T(8,128)(2,1)} %bitcast.131, pred[128,32]{1,0:T(8,128)(4,1)S(1)} %copy.51), kind=kLoop, calls=%fused_computation.6 | loop fusion | flops 8388608 | bytes 33558528 | tf_op jit(solution)/shard_map/jit(_take)/select_n | solution.py:81
  44.7 188.0 %all_to_all.10 = bf16[128,32,2048]{2,1,0:T(8,128)(2,1)S(1)} all-to-all(bf16[128,32,2048]{2,1,0:T(8,128)(2,1)S(1)} %broadcast_select_fusion), channel_id=1, replica_groups=mesh['dp'=1,'ep'=8] {'ep'}, dimensions={0} | all-to-all | bytes 33554432 | tf_op jit(solution)/shard_map/all_to_all | solution.py:82
  232.6 6.5 %copy.53 = bf16[16,8,32,2048]{3,2,1,0:T(8,128)(2,1)} copy(bf16[16,8,32,2048]{3,2,0,1:T(8,128)(2,1)S(1)} %bitcast.133) | data formatting | bytes 33554432 | tf_op jit(solution)/shard_map/transpose | solution.py:83
  239.2 28.5 %fusion.63 = f32[16,256,768]{2,1,0:T(8,128)} fusion(bf16[16,256,2048]{2,1,0:T(8,128)(2,1)} %bitcast.138, bf16[16,2048,768]{2,1,0:T(8,128)(2,1)} %param.31), kind=kOutput, calls=%fused_computation.100 | convolution fusion | flops 12884901888 | bytes 79691776 | tf_op jit(solution)/shard_map/ecd,edf->ecf/dot_general | solution.py:59
  267.7 47.7 %convolution_convert_fusion = bf16[16,256,2048]{2,1,0:T(8,128)(2,1)} fusion(bf16[16,768,2048]{2,1,0:T(8,128)(2,1)} %param.33, f32[16,256,768]{2,1,0:T(8,128)} %fusion.63, bf16[16,256,2048]{2,1,0:T(8,128)(2,1)} %bitcast.139, bf16[16,2048,768]{2,1,0:T(8,128)(2,1)} %param.32), kind=kOutput, calls=%fused_computation.7 | convolution fusion | flops 25797066752 | bytes 146800640 | tf_op jit(solution)/shard_map/ecf,efd->ecd/dot_general | solution.py:62
  315.4 14.1 %copy.54 = bf16[8,16,32,2048]{3,2,1,0:T(8,128)(2,1)} copy(bf16[8,16,32,2048]{3,2,0,1:T(8,128)(2,1)} %bitcast.140) | data formatting | bytes 33554432 | tf_op jit(solution)/shard_map/transpose | solution.py:85
  329.5 4.8 all-to-all-start.1
  334.3 0.1 copy.48
  334.5 0.6 convert_element_type.119
  335.1 0.6 convert_element_type.130
  335.7 0.1 copy.49
  335.9 0.1 copy.55
  336.2 2.0 convolution_convert_fusion.1
  338.2 0.8 copy.59
  339.0 1.5 fusion.62
  340.5 13.1 %gather_fusion.2 = f32[2048]{0:T(1024)S(1)} fusion(f32[256,128]{1,0:T(8,128)S(1)} %fusion.62, s32[2048]{0:T(1024)S(1)} %reshape.350), kind=kCustom, calls=%fused_computation.2 | custom fusion | bytes 32768 | tf_op jit(solution)/shard_map/jit(take_along_axis)/gather | solution.py:53
  353.7 4.0 copy.60
  357.6 22.6 %copy.63 = bf16[4096,2048]{1,0:T(8,128)(2,1)} copy(bf16[4096,2048]{0,1:T(8,128)(2,1)} %bitcast.136) | data formatting | bytes 33554432 | tf_op jit(solution)/shard_map/dot_general | solution.py:33
  380.3 0.3 multiply_cosine_fusion
  380.6 8.4 %convolution_bitcast_fusion = f32[1,256,32,128]{1,3,2,0:T(8,128)S(1)} fusion(bf16[32,128,2048]{2,1,0:T(8,128)(2,1)} %bitcast.137, bf16[1,256,2048]{2,1,0:T(8,128)(2,1)S(1)} %copy-done.2, f32[2048]{0:T(1024)S(1)} %copy-done.10, f32[256]{0:T(256)S(1)} %copy-done.12), kind=kOutput, calls=%fused_computation.35 | convolution fusion | flops 4297064448 | bytes 22029312 | tf_op jit(solution)/shard_map/dot_general | solution.py:33
  389.0 0.6 subtract_convert_fusion
  389.7 1.8 copy.44
  391.4 2.0 copy.43
  393.5 0.1 fusion.58
  393.6 0.2 fusion.50
  393.8 2.6 convolution_bitcast_fusion.1
  396.5 2.6 fusion.3
  399.2 1.8 fusion.2
  401.0 3.6 fusion.26
  404.6 0.5 slice-done.2
  405.1 1.3 slice-done.3
  406.4 6.3 %fusion.18 = (f32[256]{0:T(256)S(1)}, bf16[256,2048]{1,0:T(8,128)(2,1)S(1)}) fusion(bf16[256,4096]{0,1:T(8,128)(2,1)} %bitcast.143, bf16[4096,2048]{1,0:T(8,128)(2,1)S(1)} %bitcast.135, bf16[1,256,2048]{2,1,0:T(8,128)(2,1)S(1)} %copy-done.2), kind=kOutput, calls=%fused_computation.38 | convolution fusion | flops 4298113024 | bytes 20972544 | tf_op jit(solution)/shard_map/dot_general | solution.py:42
  412.7 0.1 fusion.49
  412.9 14.6 %fusion.31 = f32[256,6144]{1,0:T(8,128)} fusion(bf16[2048,6144]{1,0:T(8,128)(2,1)} %param.26, bf16[256,2048]{1,0:T(8,128)(2,1)S(1)} %get-tuple-element.18, f32[2048]{0:T(1024)S(1)} %copy-done.9, f32[256]{0:T(256)S(1)} %add_rsqrt_fusion), kind=kOutput, calls=%fused_computation.49 | convolution fusion | flops 6444548096 | bytes 32515072 | tf_op jit(solution)/shard_map/dot_general | solution.py:44
  427.4 90.9 %all-to-all-done.1 = bf16[128,32,2048]{2,1,0:T(8,128)(2,1)} async-done(((bf16[128,32,2048]{2,1,0:T(8,128)(2,1)}), bf16[128,32,2048]{2,1,0:T(8,128)(2,1)}, u32[]{:S(2)}, u32[]{:S(2)}) %all-to-all-start.1) | async-done | bytes 16777248 | tf_op jit(solution)/shard_map/all_to_all | solution.py:86
  518.3 50.4 %gather_fusion.1 = bf16[2048,2048]{1,0:T(8,128)(2,1)} fusion(bf16[128,32,2048]{2,1,0:T(8,128)(2,1)} %all-to-all-done.1, s32[2048]{0:T(1024)S(1)} %reshape.344), kind=kCustom, calls=%fused_computation.1 | custom fusion | bytes 16793600 | tf_op jit(solution)/shard_map/gather | solution.py:87
  568.6 12.5 %fusion = f32[256,2048]{1,0:T(8,128)} fusion(bf16[2048,2048]{1,0:T(8,128)(2,1)} %gather_fusion.1, f32[256,8]{1,0:T(8,128)S(1)} %fusion.49), kind=kLoop, calls=%fused_computation.5 | loop fusion | flops 12058624 | bytes 10493952 | tf_op jit(solution)/shard_map/reduce_sum | solution.py:88
  581.2 24.0 %fusion.15 = bf16[1,256,2048]{2,1,0:T(8,128)(2,1)} fusion(f32[256,2048]{1,0:T(8,128)} %fusion, bf16[6144,2048]{1,0:T(8,128)(2,1)} %param.28, bf16[2048,6144]{1,0:T(8,128)(2,1)} %param.27, f32[256,6144]{1,0:T(8,128)} %fusion.31, bf16[256,2048]{1,0:T(8,128)(2,1)S(1)} %get-tuple-element.18, f32[2048]{0:T(1024)S(1)} %copy-done.9, f32[256]{0:T(256)S(1)} %add_rsqrt_fusion), kind=kOutput, calls=%fused_computation.34 | convolution fusion | flops 12898533376 | bytes 60826624 | tf_op jit(solution)/shard_map/dot_general | solution.py:45
  (55 shorter events, 1.0 us)
Async XLA Ops:
  0.0 336.1 %copy-start = (bf16[2048,512]{1,0:T(8,128)(2,1)S(1)}, bf16[2048,512]{1,0:T(8,128)(2,1)}, u32[]{:S(2)}) copy-start(bf16[2048,512]{1,0:T(8,128)(2,1)} %param.23) | copy-start | bytes 6291460
  12.9 23.4 %copy-start.11 = (f32[256]{0:T(256)}, f32[256]{0:T(256)S(1)}, u32[]{:S(2)}) copy-start(f32[256]{0:T(256)S(1)} %add_rsqrt_fusion.1) | copy-start | bytes 3076
  329.5 4.8 copy-start.6
  329.5 5.0 copy-start.13
  329.5 5.6 copy-start.14
  329.5 6.2 %copy-start.8 = (s32[256,8,1]{0,1,2:T(8,128)S(1)}, s32[256,8,1]{0,1,2:T(8,128)}, u32[]{:S(2)}) copy-start(s32[256,8,1]{0,1,2:T(8,128)} %get-tuple-element.9) | copy-start | bytes 24580
  329.5 6.4 %copy-start.7 = (s32[256,8,1]{0,1,2:T(8,128)S(1)}, s32[256,8,1]{0,1,2:T(8,128)}, u32[]{:S(2)}) copy-start(s32[256,8,1]{0,1,2:T(8,128)} %get-tuple-element.10) | copy-start | bytes 24580
  329.5 188.8 %all-to-all-start.1 = ((bf16[128,32,2048]{2,1,0:T(8,128)(2,1)}), bf16[128,32,2048]{2,1,0:T(8,128)(2,1)}, u32[]{:S(2)}, u32[]{:S(2)}) async-start(bf16[128,32,2048]{2,1,0:T(8,128)(2,1)} %bitcast.132), calls=%async_computation.1 | async-start | bytes 33554432 | tf_op jit(solution)/shard_map/all_to_all | solution.py:86
  357.6 23.0 %copy-start.2 = (bf16[1,256,2048]{2,1,0:T(8,128)(2,1)S(1)}, bf16[1,256,2048]{2,1,0:T(8,128)(2,1)}, u32[]{:S(2)}) copy-start(bf16[1,256,2048]{2,1,0:T(8,128)(2,1)} %param.17) | copy-start | bytes 3145732
  357.6 23.0 %copy-start.10 = (f32[2048]{0:T(1024)S(1)}, f32[2048]{0:T(1024)}, u32[]{:S(2)}) copy-start(f32[2048]{0:T(1024)} %convert_element_type.119) | copy-start | bytes 24580
  357.6 23.0 %copy-start.12 = (f32[256]{0:T(256)S(1)}, f32[256]{0:T(256)}, u32[]{:S(2)}) copy-start(f32[256]{0:T(256)} %copy-done.11) | copy-start | bytes 3076
  393.4 3.1 copy-start.3
  393.5 3.1 copy-start.4
  399.1 1.8 copy-start.5
  399.2 5.5 slice-start
  401.0 3.7 slice-start.1
  401.0 4.1 slice-start.2
  401.0 5.4 slice-start.3
  406.4 6.4 %copy-start.9 = (f32[2048]{0:T(1024)S(1)}, f32[2048]{0:T(1024)}, u32[]{:S(2)}) copy-start(f32[2048]{0:T(1024)} %convert_element_type.130) | copy-start | bytes 24580
  581.2 24.0 %copy-start.1 = (bf16[2048,512]{1,0:T(8,128)(2,1)S(1)}, bf16[2048,512]{1,0:T(8,128)(2,1)}, u32[]{:S(2)}) copy-start(bf16[2048,512]{1,0:T(8,128)(2,1)} %param.23) | copy-start | bytes 6291460
where the time goes:
time: 614 us; the launch traced here: 606 us
  blocking collectives  188 us (31%)
  local copies, waits for them, and re-layouts  147 us (24%)
  matrix products  142 us (23%)
  waiting for transfers between devices  90.9 us (15%)
  other arithmetic  32 us (5%)
    all_to_all x1, blocking collectives, local(): recv = lax.all_to_all(send, 'ep', 0, 0, tiled=True)  188 us
    all_to_all x1, waiting for transfers between devices, local(): back = lax.all_to_all(y, 'ep', 0, 0, tiled=True)  90.9 us
    gather x1, local copies, waits for them, and re-layouts, local(): yg = back[ix, sl]  50.4 us
    dot_general x1, matrix products, _experts(): jnp.einsum('ecf,efd->ecd', hid, ue2, preferred_element_type=f32)  47.7 us
    dot_general x1, matrix products, _experts(): h1 = jnp.einsum('ecd,edf->ecf', x, ue1, preferred_element_type=f32)  28.5 us
    dot_general x1, matrix products, _dense(): return a.astype(f32) + jnp.dot(hid, w2, preferred_element_type=f32)  24 us
    dot_general x1, local copies, waits for them, and re-layouts, _dense(): jnp.dot(x, wq, preferred_element_type=f32).reshape(b, s, nh, HEAD)  22.6 us
    gather x1, local copies, waits for them, and re-layouts, local(): send = jnp.take(u, tok, axis=0, mode='fill', fill_value=0)  20.9 us
  transfers between devices with their start and end apart: 1, of which 1 were waited for; matrix products, arithmetic and copies ran while one was open for 15% of the time, Pallas kernels for 0%

commit v1 on v0

v1 whole, which is shorter than its diff:
```python
import jax
import jax.numpy as jnp
from jax import lax
from jax.experimental import pallas as pl
from jax.experimental.pallas import tpu as pltpu
from jax.sharding import PartitionSpec as P

HEAD = 128
EPS = 1e-6
ROPE_BASE = 10000.0
MESH = pl.DeviceIdType.MESH
F32 = jnp.float32
BF = jnp.bfloat16
VMEM_LIMIT = 62 * 1024 * 1024


def _peers():
    me = lax.axis_index('ep')
    core, x, y = me % 2, (me // 2) % 2, me // 4
    out = []
    for r in range(4):
        px = 1 - x if r % 2 else x
        py = 1 - y if r // 2 else y
        for p in range(2):
            pc = 1 - core if p else core
            out.append((py * 2 + px) * 2 + pc)
    return out


def _dot(a, b):
    return jnp.dot(a, b, preferred_element_type=F32)


def _rms_rows(x, w):
    xf = x.astype(F32)
    r = lax.rsqrt(jnp.mean(xf * xf, axis=-1, keepdims=True) + EPS)
    return (xf * r * w.astype(F32)).astype(BF)


def _dispatch(meta, u, e0, cap, rows, x_ref, gt_ref):
    k = meta.shape[0] // 3
    t = meta.shape[1]
    idx, slot, g = meta[:k], meta[k:2 * k], meta[2 * k:3 * k]
    local = idx - e0
    key = jnp.where((local >= 0.0) & (local < rows // cap), local * cap + slot, -1.0)
    step = 128
    for b in range(rows // step):
        row = lax.broadcasted_iota(jnp.int32, (step, t), 0).astype(F32) + float(b * step)
        d = jnp.zeros((step, t), F32)
        gt = jnp.zeros((step, t), F32)
        for j in range(k):
            hit = row == key[j:j + 1, :]
            d = jnp.where(hit, 1.0, d)
            gt = jnp.where(hit, g[j:j + 1, :], gt)
        hi = gt.astype(BF)
        rest = gt - hi.astype(F32)
        mid = rest.astype(BF)
        lo = (rest - mid.astype(F32)).astype(BF)
        gt_ref[0, pl.ds(b * step, step), :] = hi
        gt_ref[0, pl.ds(rows + b * step, step), :] = mid
        gt_ref[0, pl.ds(2 * rows + b * step, step), :] = lo
        x_ref[0, pl.ds(b * step, step), :] = _dot(d.astype(BF), u).astype(BF)


ATT = 8
CH = 4


def _gather_kernel(cap, h0_ref, is_ref, na_ref, nf_ref, nm_ref, cos_ref, sin_ref, wr_ref, wq_ref, wk_ref, wv_ref, wo_ref,
                   x_ref, gt_ref, a_ref, z_ref,
                   u, meta, xa, acc, kb, vb, ob, own_s, own_r, part_s, part_r, fwd_s, fwd_r, rel_s, rel_r, met_s, met_r):
    i = pl.program_id(0)
    peers = _peers()
    t = h0_ref.shape[0]
    rows = x_ref.shape[1]
    hb = wq_ref.shape[1] // HEAD
    ch = t // CH
    order = (tuple(range(CH)), tuple(range(CH // 2, CH)) + tuple(range(CH // 2)))

    def rc(src, dst, ss, rs, peer):
        return pltpu.make_async_remote_copy(src_ref=src, dst_ref=dst, send_sem=ss, recv_sem=rs,
                                            device_id={'ep': peer}, device_id_type=MESH)

    def own(link, n):
        sl = pl.ds(order[link][n] * ch, ch)
        return rc(u.at[0, sl], u.at[2 + 2 * link, sl], own_s.at[link, n], own_r.at[link, n], peers[2 + 2 * link])

    def part():
        return rc(u.at[0], u.at[1], part_s.at[0], part_r.at[0], peers[1])

    def fwd(link, n):
        sl = pl.ds(order[link][n] * ch, ch)
        return rc(u.at[2 + 2 * link, sl], u.at[3 + 2 * link, sl], fwd_s.at[link, n], fwd_r.at[link, n], peers[1])

    def relay(link, n):
        sl = pl.ds(order[link][n] * ch, ch)
        return rc(u.at[2 + 2 * link, sl], u.at[6, sl], rel_s.at[link, n], rel_r.at[link, n], peers[4 - 2 * link])

    def fwd3(link, n):
        sl = pl.ds(order[link][n] * ch, ch)
        return rc(u.at[6, sl], u.at[7, sl], fwd_s.at[2 + link, n], fwd_r.at[2 + link, n], peers[1])

    def met(s):
        return rc(meta.at[0], meta.at[s], met_s.at[s], met_r.at[s], peers[s])

    def pass_on(n):
        for link in range(2):
            own(link, n).wait_recv()
            if n < CH // 2:
                relay(link, n).start()
            fwd(link, n).start()

    @pl.when(i == 0)
    def _():
        barrier = pltpu.get_barrier_semaphore()
        for s in range(1, 8):
            pl.semaphore_signal(barrier, inc=1, device_id={'ep': peers[s]}, device_id_type=MESH)
        uu = _rms_rows(h0_ref[...], nm_ref[...])
        u[0] = uu
        pl.semaphore_wait(barrier, 7)
        for n in range(CH):
            for link in range(2):
                own(link, n).start()
        part().start()
        xa[...] = _rms_rows(h0_ref[...], na_ref[...])
        k = is_ref.shape[0] // 2
        lt = _dot(uu, wr_ref[...]).T
        it = is_ref[...]
        ids = lax.broadcasted_iota(jnp.int32, lt.shape, 0)
        sel = [jnp.sum(jnp.where(ids == it[j:j + 1, :], lt, 0.0), axis=0, keepdims=True) for j in range(k)]
        lg = jnp.concatenate(sel, axis=0)
        ex = jnp.exp(lg - jnp.max(lg, axis=0, keepdims=True))
        meta[0, 0:2 * k, :] = it.astype(F32)
        meta[0, 2 * k:3 * k, :] = ex / jnp.sum(ex, axis=0, keepdims=True)
        acc[...] = h0_ref[...].astype(F32)

    @pl.when(i == 1)
    def _():
        for s in range(1, 8):
            met(s).start()

    @pl.when(i < ATT)
    def _():
        x = xa[...]
        cos, sin = cos_ref[...], sin_ref[...]

        def rope(v):
            return (v * cos + pltpu.roll(v, HEAD // 2, 1) * sin).astype(BF)

        @pl.when(i % 2 == 0)
        def _():
            kb[...] = rope(_dot(x, wk_ref[...]))
            vb[...] = _dot(x, wv_ref[...]).astype(BF)

        q = _dot(x, wq_ref[...])
        causal = lax.broadcasted_iota(jnp.int32, (t, t), 0) >= lax.broadcasted_iota(jnp.int32, (t, t), 1)
        kk, vv = kb[...], vb[...]
        for h in range(hb):
            qh = rope(q[:, h * HEAD:(h + 1) * HEAD])
            s = lax.dot_general(qh, kk, (((1,), (1,)), ((), ())), preferred_element_type=F32) * HEAD ** -0.5
            s = jnp.where(causal, s, -jnp.inf)
            ex = jnp.exp(s - jnp.max(s, axis=1, keepdims=True))
            p = (ex / jnp.sum(ex, axis=1, keepdims=True)).astype(BF)
            ob[:, h * HEAD:(h + 1) * HEAD] = _dot(p, vv).astype(BF)
        acc[...] += _dot(ob[...], wo_ref[...])

    for n in range(CH):
        @pl.when(i == 2 * n + 2)
        def _(n=n):
            pass_on(n)

    @pl.when(i == ATT)
    def _():
        a = acc[...].astype(BF)
        a_ref[...] = a
        z_ref[...] = _rms_rows(a, nf_ref[...])

    for s in range(8):
        @pl.when(i == ATT + s)
        def _(s=s):
            if s == 1:
                part().wait_recv()
            if s in (3, 5):
                for n in range(CH):
                    fwd((s - 3) // 2, n).wait_recv()
            if s == 6:
                for n in range(CH // 2):
                    for link in range(2):
                        relay(link, n).wait_recv()
                        fwd3(link, n).start()
            if s == 7:
                for n in range(CH // 2):
                    for link in range(2):
                        fwd3(link, n).wait_recv()
            if s:
                met(s).wait_recv()
            e0 = lax.axis_index('ep') * (rows // cap)
            _dispatch(meta[s], u[s], e0.astype(F32), cap, rows, x_ref, gt_ref)
            if s == 7:
                part().wait_send()
                for link in range(2):
                    for n in range(CH):
                        own(link, n).wait_send()
                        fwd(link, n).wait_send()
                        if n < CH // 2:
                            relay(link, n).wait_send()
                            fwd3(link, n).wait_send()
                for q in range(1, 8):
                    met(q).wait_send()


def _gather(h0, ist, na, nf, nm, cos, sin, wr, wq, wk, wv, wo, el, cap):
    t, d = h0.shape
    rows = el * cap
    qb = wq.shape[1] // ATT
    kv = wk.shape[1] // HEAD
    full = lambda a: pl.BlockSpec(a.shape, lambda i: (0,) * a.ndim)
    att = lambda i: jnp.minimum(i, ATT - 1)
    src = lambda i: jnp.maximum(i - ATT, 0)
    dma = pltpu.SemaphoreType.DMA
    return pl.pallas_call(
        lambda *refs: _gather_kernel(cap, *refs),
        grid=(ATT + 8,),
        in_specs=[full(h0), full(ist), full(na), full(nf), full(nm), full(cos), full(sin), full(wr),
                  pl.BlockSpec((d, qb), lambda i: (0, att(i))),
                  pl.BlockSpec((d, HEAD), lambda i: (0, att(i) * kv // ATT)),
                  pl.BlockSpec((d, HEAD), lambda i: (0, att(i) * kv // ATT)),
                  pl.BlockSpec((qb, d), lambda i: (att(i), 0))],
        out_specs=[pl.BlockSpec((1, rows, d), lambda i: (src(i), 0, 0)),
                   pl.BlockSpec((1, 3 * rows, t), lambda i: (src(i), 0, 0)),
                   pl.BlockSpec((t, d), lambda i: (0, 0)), pl.BlockSpec((t, d), lambda i: (0, 0))],
        out_shape=[jax.ShapeDtypeStruct((8, rows, d), BF), jax.ShapeDtypeStruct((8, 3 * rows, t), BF),
                   jax.ShapeDtypeStruct((t, d), BF), jax.ShapeDtypeStruct((t, d), BF)],
        scratch_shapes=[pltpu.VMEM((8, t, d), BF), pltpu.VMEM((8, 3 * ist.shape[0] // 2, t), F32),
                        pltpu.VMEM((t, d), BF), pltpu.VMEM((t, d), F32),
                        pltpu.VMEM((t, HEAD), BF), pltpu.VMEM((t, HEAD), BF), pltpu.VMEM((t, qb), BF),
                        dma((2, CH)), dma((2, CH)), dma((1,)), dma((1,)), dma((4, CH)), dma((4, CH)),
                        dma((2, CH)), dma((2, CH)), dma((8,)), dma((8,))],
        compiler_params=pltpu.CompilerParams(dimension_semantics=('arbitrary',), collective_id=0, has_side_effects=True,
                                             vmem_limit_bytes=VMEM_LIMIT),
        name='gather_attention',
    )(h0, ist, na, nf, nm, cos, sin, wr, wq, wk, wv, wo)


def _up_kernel(x_ref, w1_ref, w3_ref, o_ref):
    x = x_ref[...].reshape(o_ref.shape[1], x_ref.shape[-1])
    h1 = _dot(x, w1_ref[0])
    h3 = _dot(x, w3_ref[0])
    o_ref[0] = (h1 * jax.nn.sigmoid(h1) * h3).astype(BF)


def _up(x, ue1, ue3, cap):
    el, d, fe = ue1.shape
    m = 8 * cap
    w = pl.BlockSpec((1, d, fe), lambda e: (e, 0, 0))
    return pl.pallas_call(
        _up_kernel,
        grid=(el,),
        in_specs=[pl.BlockSpec((8, 1, cap, d), lambda e: (0, e, 0, 0)), w, w],
        out_specs=pl.BlockSpec((1, m, fe), lambda e: (e, 0, 0)),
        out_shape=jax.ShapeDtypeStruct((el, m, fe), BF),
        compiler_params=pltpu.CompilerParams(dimension_semantics=('arbitrary',), vmem_limit_bytes=VMEM_LIMIT),
        name='expert_up',
    )(x.reshape(8, el, cap, d), ue1, ue3)


NC = 8
FS = 24
FLAG = 2
LANES = 128
POS = ((0, 2, 1, 3), (0, 1, 2, 3))


def _down_kernel(cap, hid_ref, gt_ref, a_ref, z_ref, ue2_ref, w1_ref, w3_ref, w2_ref, out_ref,
                 yb, mo, mp, r0, r1, r2, acc, d_s, d_r, credit, p1_s, p1_r, p2_s, p2_r):
    i = pl.program_id(0)
    peers = _peers()
    el, m, fe = hid_ref.shape
    half = ue2_ref.shape[0]
    rows = el * cap

    def rc(src, dst, ss, rs, peer):
        return pltpu.make_async_remote_copy(src_ref=src, dst_ref=dst, send_sem=ss, recv_sem=rs,
                                            device_id={'ep': peer}, device_id_type=MESH)

    def pair(c):
        return rc(mo.at[c % 2], r0.at[c % 2], d_s.at[c % 2], d_r.at[c % 2], peers[1])

    def first(c, b):
        return rc(mp.at[c, b, pl.ds(2, 2)], r1.at[c, b], p1_s.at[c, b], p1_r.at[c, b], peers[2 + 2 * b])

    def second(c, b):
        return rc(mp.at[c, b, 1], r2.at[c, b], p2_s.at[c, b], p2_r.at[c, b], peers[4 - 2 * b])

    @pl.when(i == 0)
    def _():
        barrier = pltpu.get_barrier_semaphore()
        for s in (1, 2, 4):
            pl.semaphore_signal(barrier, inc=1, device_id={'ep': peers[s]}, device_id_type=MESH)
        acc[...] = a_ref[...].astype(F32)
        pl.semaphore_wait(barrier, 3)

    @pl.when(i < 2 * NC)
    def _():
        base = (i % 2) * half
        for e in range(half):
            y = _dot(hid_ref[base + e], ue2_ref[e]).astype(BF)
            for s in range(8):
                yb[s, pl.ds(pl.multiple_of((base + e) * cap, cap), cap), :] = y[s * cap:(s + 1) * cap]

    @pl.when((i % 2 == 0) & (i >= 2) & (i <= 2 * NC))
    def _():
        c = i // 2 - 1
        pair(c).wait()
        mp[c] = mp[c] + r0[c % 2]

        @pl.when(c < NC - 2)
        def _():
            pl.semaphore_signal(credit, inc=1, device_id={'ep': peers[1]}, device_id_type=MESH)

        for b in range(2):
            first(c, b).start()

    @pl.when((i % 2 == 1) & (i < 2 * NC))
    def _():
        c = i // 2
        for s in range(8):
            y = yb[s]
            v = None
            for q in range(3):
                w = lax.dot_general(gt_ref[s, pl.ds(q * rows, rows), :], y, (((0,), (0,)), ((), ())),
                                    preferred_element_type=F32)
                v = w if v is None else v + w
            for b in range(2):
                dst = v[:, b * LANES:(b + 1) * LANES]
                if s % 2:
                    mo[c % 2, b, POS[b][s // 2]] = dst
                else:
                    mp[c, b, POS[b][s // 2]] = dst

        @pl.when(c >= 2)
        def _():
            pl.semaphore_wait(credit, 1)

        pair(c).start()

    @pl.when(i >= FLAG)
    def _():
        z = z_ref[...]
        h1 = _dot(z, w1_ref[...])
        h3 = _dot(z, w3_ref[...])
        acc[...] += _dot((h1 * jax.nn.sigmoid(h1) * h3).astype(BF), w2_ref[...])

    @pl.when((i % 2 == 1) & (i >= 5) & (i < 2 * NC + 5))
    def _():
        c = (i - 5) // 2
        for b in range(2):
            first(c, b).wait_recv()
            mp[c, b, pl.ds(0, 2)] = mp[c, b, pl.ds(0, 2)] + r1[c, b]
            second(c, b).start()

    @pl.when(i == FS + FLAG - 1)
    def _():
        for c in range(NC):
            for b in range(2):
                second(c, b).wait_recv()
                col = pl.ds((2 * c + b) * LANES, LANES)
                out_ref[:, col] = (acc[:, col] + (mp[c, b, 0] + r2[c, b])).astype(BF)
        for c in range(NC):
            for b in range(2):
                first(c, b).wait_send()
                second(c, b).wait_send()


def _down(hid, gt, a, z, ue2, w1, w3, w2, cap):
    el, m, fe = hid.shape
    t, d = a.shape
    nb = d // NC
    fb = w1.shape[1] // FS
    full = lambda v: pl.BlockSpec(v.shape, lambda i: (0,) * v.ndim, pipeline_mode=pl.Buffered(1))
    ci = lambda i: jnp.minimum(i, 2 * NC - 1)
    fi = lambda i: jnp.clip(i - FLAG, 0, FS - 1)
    dma = pltpu.SemaphoreType.DMA
    return pl.pallas_call(
        lambda *refs: _down_kernel(cap, *refs),
        grid=(FS + FLAG,),
        in_specs=[full(hid), full(gt), full(a), full(z),
                  pl.BlockSpec((el // 2, fe, nb), lambda i: (ci(i) % 2, 0, ci(i) // 2)),
                  pl.BlockSpec((d, fb), lambda i: (0, fi(i))),
                  pl.BlockSpec((d, fb), lambda i: (0, fi(i))),
                  pl.BlockSpec((fb, d), lambda i: (fi(i), 0))],
        out_specs=pl.BlockSpec((t, d), lambda i: (0, 0)),
        out_shape=jax.ShapeDtypeStruct((t, d), BF),
        scratch_shapes=[pltpu.VMEM((8, el * cap, nb), BF),
                        pltpu.VMEM((2, 2, 4, t, LANES), F32), pltpu.VMEM((NC, 2, 4, t, LANES), F32),
                        pltpu.VMEM((2, 2, 4, t, LANES), F32), pltpu.VMEM((NC, 2, 2, t, LANES), F32),
                        pltpu.VMEM((NC, 2, t, LANES), F32), pltpu.VMEM((t, d), F32),
                        dma((2,)), dma((2,)), pltpu.SemaphoreType.REGULAR,
                        dma((NC, 2)), dma((NC, 2)), dma((NC, 2)), dma((NC, 2))],
        compiler_params=pltpu.CompilerParams(dimension_semantics=('arbitrary',), collective_id=1, has_side_effects=True,
                                             vmem_limit_bytes=VMEM_LIMIT),
        name='expert_down_ffn',
    )(hid, gt, a, z, ue2, w1, w3, w2)


def solution(mesh):
    G = mesh.shape['ep']

    def local(h0, idx, slot, na, wq, wk, wv, wo, nf, w1, w3, w2, nm, wr, ue1, ue3, ue2):
        b, s, d = h0.shape
        k = idx.shape[-1]
        el = ue1.shape[0]
        cap = 2 * s * k // (el * G)
        pos = jnp.arange(s).astype(F32)
        inv = ROPE_BASE ** (-2.0 * jnp.arange(HEAD // 2).astype(F32) / HEAD)
        ang = pos[:, None] * inv[None, :]
        cos, sin = jnp.cos(ang), jnp.sin(ang)
        cos = jnp.concatenate([cos, cos], axis=1)
        sin = jnp.concatenate([-sin, sin], axis=1)
        ist = jnp.concatenate([idx.reshape(s, k).T, slot.reshape(s, k).T], axis=0)
        h = h0.reshape(s, d)
        x, gt, a, z = _gather(h, ist, na.reshape(1, d), nf.reshape(1, d), nm.reshape(1, d), cos, sin, wr, wq, wk, wv, wo,
                              el, cap)
        hid = _up(x, ue1, ue3, cap)
        return _down(hid, gt, a, z, ue2, w1, w3, w2, cap).reshape(b, s, d)

    rows_spec = P(('dp', 'ep'))
    in_specs = (rows_spec,) * 3 + (P(),) * 11 + (P('ep'),) * 3
    return jax.shard_map(local, mesh=mesh, in_specs=in_specs, out_specs=rows_spec, check_vma=False)
```

time: 614 us -> 195 us (0.32); the launches traced: 606 us -> 195 us
  blocking collectives: 188 us -> 0 us
  Pallas kernels: 0 us -> 186 us
  matrix products: 142 us -> 0 us
  local copies, waits for them, and re-layouts: 147 us -> 6.16 us
  waiting for transfers between devices: 90.9 us -> 0 us
  other arithmetic: 32 us -> 2.7 us
    all_to_all x1 -> x0, blocking collectives: 188 us -> none  [local(): recv = lax.all_to_all(send, 'ep', 0, 0, tiled=True)]
    pallas_call x0 -> x3, Pallas kernels: none -> 186 us  [the longest x1 91 us: _down(): pl.pallas_call(lambda *refs: _down_kernel(cap, *refs), grid=(FS + FLAG,),...]
    dot_general x11 -> x0, matrix products: 142 us -> none  [the longest x1 47.7 us: _experts(): jnp.einsum('ecf,efd->ecd', hid, ue2, preferred_element_type=f32)]
    all_to_all x1 -> x0, waiting for transfers between devices: 90.9 us -> none  [local(): back = lax.all_to_all(y, 'ep', 0, 0, tiled=True)]
    gather x6 -> x0, local copies, waits for them, and re-layouts: 84.6 us -> none  [the longest x1 50.4 us: local(): yg = back[ix, sl]]
    dot_general x2 -> x0, local copies, waits for them, and re-layouts: 26.6 us -> none  [the longest x1 22.6 us: _dense(): jnp.dot(x, wq, preferred_element_type=f32).reshape(b, s, nh, HEAD)]
    transpose x2 -> x0, local copies, waits for them, and re-layouts: 20.6 us -> none  [the longest x1 14.1 us: local(): y = y.reshape(el, G, cap, d).transpose(1, 0, 2, 3).reshape(e, cap, d)]
    reduce_sum x4 -> x0, other arithmetic: 16 us -> none  [the longest x1 12.5 us: local(): m = jnp.sum(g[..., None] * yg.astype(f32), axis=1)]
  transfers between devices with their start and end apart: 1 -> 0, of which waited for: 1 -> 0; matrix products, arithmetic and copies ran while one was open for 15% -> 0% of each run, Pallas kernels for 0% -> 0%
where the time goes in v1:
time: 195 us
  Pallas kernels  186 us (95%)
  local copies, waits for them, and re-layouts  6.16 us (3%)
  other arithmetic  2.7 us (1%)
    pallas_call x1, Pallas kernels, _down(): pl.pallas_call(lambda *refs: _down_kernel(cap, *refs), grid=(FS + FLAG,),...  91 us
    pallas_call x1, Pallas kernels, _gather(): pl.pallas_call(lambda *refs: _gather_kernel(cap, *refs), grid=(ATT + 8,),...  50.5 us
    pallas_call x1, Pallas kernels, _up(): pl.pallas_call(_up_kernel, grid=(el,), in_specs=[pl.BlockSpec((8, 1, cap,...  44.8 us

profile of v1, /device:TPU:0, one launch (start us, length us, event | category | flops | bytes accessed | tf_op | source)
XLA Modules:
  0.0 195.2 jit_solution(7407825708124167285)
XLA Ops:
  0.0 1.3 reshape.37.refs_2_
  1.3 1.3 reshape.38.refs_3_
  2.6 1.3 reshape.39.refs_4_
  3.9 1.3 pad_add_fusion.refs_1_
  5.2 0.5 fusion
  5.7 0.8 pad_maximum_fusion
  6.6 50.5 %gather_attention.1 = (bf16[8,512,2048]{2,1,0:T(8,128)(2,1)}, bf16[8,1536,256]{2,1,0:T(8,128)(2,1)}, bf16[256,2048]{1,0:T(8,128)(2,1)}, bf16[256,2048]{1,0:T(8,128)(2,1)}) custom-call(bf16[256,2048]{1,0:T(8,128)(2,1)} %bitcast.11, s32[16,256]{1,0:T(8,128)} %pad_add_fusion.refs_1_, bf16[1,2048]{1,0:T(2,128)(2,1)} %reshape.37.refs_2_, ...), custom_call_target="tpu_custom_call" | custom-call | tf_op jit(solution)/shard_map/gather_attention/pallas_call | solution.py:221
  57.0 44.8 %expert_up.1.refs_0_ = bf16[16,256,768]{2,1,0:T(8,128)(2,1)} custom-call(bf16[8,16,32,2048]{3,2,1,0:T(8,128)(2,1)} %bitcast.9, bf16[16,2048,768]{2,1,0:T(8,128)(2,1)} %w1_ref.1, bf16[16,2048,768]{2,1,0:T(8,128)(2,1)} %w3_ref.1), custom_call_target="tpu_custom_call" | custom-call | tf_op jit(solution)/shard_map/expert_up/pallas_call | solution.py:256
  101.9 91.0 %expert_down_ffn.1 = bf16[256,2048]{1,0:T(8,128)(2,1)} custom-call(bf16[16,256,768]{2,1,0:T(8,128)(2,1)} %expert_up.1.refs_0_, bf16[8,1536,256]{2,1,0:T(8,128)(2,1)} %get-tuple-element.10.refs_1_, bf16[256,2048]{1,0:T(8,128)(2,1)} %get-tuple-element.11.refs_2_, bf16[256,2048]{1,0:T(8,128)(2,1)} %get-tuple-element.12.refs_3_, bf16[16,768,2048]{2,1,0:T(8,128)(2,1)} %refs_4_.1, ...), custom_call_target="tpu_custom_call" | custom-call | tf_op jit(solution)/shard_map/expert_down_ffn/pallas_call | solution.py:384
  192.8 2.3 %copy.19 = bf16[1,256,2048]{2,1,0:T(8,128)(2,1)} copy(bf16[1,256,2048]{2,1,0:T(8,128)(2,1)} %bitcast.10) | data formatting | bytes 2097152
  (2 shorter events, 0.0 us)

commit v2 on v1

v2 whole, which is shorter than its diff:
```python
import jax
import jax.numpy as jnp
import numpy as np
from jax import lax
from jax.experimental import pallas as pl
from jax.experimental.pallas import tpu as pltpu
from jax.sharding import PartitionSpec as P

HEAD = 128
EPS = 1e-6
ROPE_BASE = 10000.0
MESH = pl.DeviceIdType.MESH
F32 = jnp.float32
BF = jnp.bfloat16
VMEM_LIMIT = 62 * 1024 * 1024


def _peers():
    me = lax.axis_index('ep')
    core, x, y = me % 2, (me // 2) % 2, me // 4
    out = []
    for r in range(4):
        px = 1 - x if r % 2 else x
        py = 1 - y if r // 2 else y
        for p in range(2):
            pc = 1 - core if p else core
            out.append((py * 2 + px) * 2 + pc)
    return out


def _tables(t):
    inv = ROPE_BASE ** (-2.0 * np.arange(HEAD // 2, dtype=np.float64) / HEAD)
    ang = np.arange(t, dtype=np.float64)[:, None] * inv[None, :]
    cos, sin = np.cos(ang), np.sin(ang)
    return (jnp.asarray(np.concatenate([cos, cos], axis=1), F32), jnp.asarray(np.concatenate([-sin, sin], axis=1), F32))


def _dot(a, b):
    return jnp.dot(a, b, preferred_element_type=F32)


def _rms_rows(x, w):
    xf = x.astype(F32)
    r = lax.rsqrt(jnp.mean(xf * xf, axis=-1, keepdims=True) + EPS)
    return (xf * r * w.astype(F32)).astype(BF)


def _dispatch(meta, u, e0, cap, rows, x_ref, gt_ref):
    k = meta.shape[0] // 3
    t = meta.shape[1]
    idx, slot, g = meta[:k], meta[k:2 * k], meta[2 * k:3 * k]
    local = idx - e0
    key = jnp.where((local >= 0.0) & (local < rows // cap), local * cap + slot, -1.0)
    step = 128
    for b in range(rows // step):
        row = lax.broadcasted_iota(jnp.int32, (step, t), 0).astype(F32) + float(b * step)
        d = jnp.zeros((step, t), F32)
        gt = jnp.zeros((step, t), F32)
        for j in range(k):
            hit = row == key[j:j + 1, :]
            d = jnp.where(hit, 1.0, d)
            gt = jnp.where(hit, g[j:j + 1, :], gt)
        col = pl.ds(b * step, step)
        gt = gt.T
        hi = gt.astype(BF)
        rest = gt - hi.astype(F32)
        mid = rest.astype(BF)
        lo = (rest - mid.astype(F32)).astype(BF)
        gt_ref[0:t, col] = hi
        gt_ref[t:2 * t, col] = mid
        gt_ref[2 * t:3 * t, col] = lo
        x_ref[pl.ds(b * step, step), :] = _dot(d.astype(BF), u).astype(BF)


ATT = 8
CH = 4
RING = 3
PASS = (3, 6, 9, 11)
D0 = ATT + 1
E0 = D0 + 8


def _front_kernel(cap, h0_ref, ix_ref, sl_ref, na_ref, nm_ref, cos_ref, sin_ref, wr_ref, wq_ref, wk_ref, wv_ref,
                  wo_ref, ue1_ref, ue3_ref, hid_ref, gt_ref, a_ref,
                  u, meta, acc, kb, vb, xs, ring, own_s, own_r, part_s, part_r, fwd_s, fwd_r, rel_s, rel_r,
                  met_s, met_r, ring_s):
    i = pl.program_id(0)
    peers = _peers()
    t, d = h0_ref.shape
    rows = xs.shape[1]
    el = rows // cap
    hb = wq_ref.shape[1] // HEAD
    ch = t // CH
    order = (tuple(range(CH)), tuple(range(CH // 2, CH)) + tuple(range(CH // 2)))

    def rc(src, dst, ss, rs, peer):
        return pltpu.make_async_remote_copy(src_ref=src, dst_ref=dst, send_sem=ss, recv_sem=rs,
                                            device_id={'ep': peer}, device_id_type=MESH)

    def own(link, n):
        sl = pl.ds(order[link][n] * ch, ch)
        return rc(u.at[0, sl], u.at[2 + 2 * link, sl], own_s.at[link, n], own_r.at[link, n], peers[2 + 2 * link])

    def part():
        return rc(u.at[0], u.at[1], part_s.at[0], part_r.at[0], peers[1])

    def fwd(link, n):
        sl = pl.ds(order[link][n] * ch, ch)
        return rc(u.at[2 + 2 * link, sl], u.at[3 + 2 * link, sl], fwd_s.at[link, n], fwd_r.at[link, n], peers[1])

    def relay(link, n):
        sl = pl.ds(order[link][n] * ch, ch)
        return rc(u.at[2 + 2 * link, sl], u.at[6, sl], rel_s.at[link, n], rel_r.at[link, n], peers[4 - 2 * link])

    def fwd3(link, n):
        sl = pl.ds(order[link][n] * ch, ch)
        return rc(u.at[6, sl], u.at[7, sl], fwd_s.at[2 + link, n], fwd_r.at[2 + link, n], peers[1])

    def met(s):
        return rc(meta.at[0], meta.at[s], met_s.at[s], met_r.at[s], peers[s])

    def weights(e, j):
        return pltpu.make_async_copy((ue1_ref, ue3_ref)[j].at[e], ring.at[e % RING, j], ring_s.at[e % RING, j])

    def pass_on(n):
        for link in range(2):
            own(link, n).wait_recv()
            if n < CH // 2:
                relay(link, n).start()
            fwd(link, n).start()

    @pl.when(i == 0)
    def _():
        barrier = pltpu.get_barrier_semaphore()
        for s in range(1, 8):
            pl.semaphore_signal(barrier, inc=1, device_id={'ep': peers[s]}, device_id_type=MESH)
        uu = _rms_rows(h0_ref[...], nm_ref[...])
        u[0] = uu
        pl.semaphore_wait(barrier, 7)
        for n in range(CH):
            for link in range(2):
                own(link, n).start()
        part().start()
        for e in range(RING):
            for j in range(2):
                weights(e, j).start()
        xs[7, 0:t] = _rms_rows(h0_ref[...], na_ref[...])
        k = ix_ref.shape[1]
        lt = _dot(uu, wr_ref[...]).T
        it = ix_ref[0]
        ids = lax.broadcasted_iota(jnp.int32, lt.shape, 0)
        sel = [jnp.sum(jnp.where(ids == it[j:j + 1, :], lt, 0.0), axis=0, keepdims=True) for j in range(k)]
        lg = jnp.concatenate(sel, axis=0)
        ex = jnp.exp(lg - jnp.max(lg, axis=0, keepdims=True))
        meta[0, 0:k, :] = it.astype(F32)
        meta[0, k:2 * k, :] = sl_ref[0].astype(F32)
        meta[0, 2 * k:3 * k, :] = ex / jnp.sum(ex, axis=0, keepdims=True)
        acc[...] = h0_ref[...].astype(F32)

    @pl.when(i == 1)
    def _():
        for s in range(1, 8):
            met(s).start()

    for n in range(CH):
        @pl.when(i == PASS[n])
        def _(n=n):
            pass_on(n)

    def rope(v):
        return (v * cos_ref[...] + pltpu.roll(v, HEAD // 2, 1) * sin_ref[...]).astype(BF)

    def project():
        q = _dot(xs[7, 0:t], wq_ref[...])

        def finish():
            for h in range(hb):
                xs[6 + i % 2, t:2 * t, h * HEAD:(h + 1) * HEAD] = rope(q[:, h * HEAD:(h + 1) * HEAD])
        return finish

    def keys():
        g = (i // 2) % 2
        kb[g] = rope(_dot(xs[7, 0:t], wk_ref[...]))
        vb[g] = _dot(xs[7, 0:t], wv_ref[...]).astype(BF)

    def attend(between):
        g = ((i - 1) // 2) % 2
        kk, vv = kb[g], vb[g]
        causal = lax.broadcasted_iota(jnp.int32, (t, t), 0) >= lax.broadcasted_iota(jnp.int32, (t, t), 1)
        sc = [lax.dot_general(xs[6 + (i - 1) % 2, t:2 * t, h * HEAD:(h + 1) * HEAD], kk, (((1,), (1,)), ((), ())),
                              preferred_element_type=F32) for h in range(hb)]
        finish = between()
        o = []
        for h in range(hb):
            s = jnp.where(causal, sc[h] * HEAD ** -0.5, -jnp.inf)
            ex = jnp.exp(s - jnp.max(s, axis=1, keepdims=True))
            p = (ex / jnp.sum(ex, axis=1, keepdims=True)).astype(BF)
            o.append(_dot(p, vv).astype(BF))
        finish()
        acc[...] += _dot(jnp.concatenate(o, axis=1), wo_ref[...])

    @pl.when((i < ATT) & (i % 2 == 0))
    def _():
        keys()

    @pl.when(i == 0)
    def _():
        project()()

    @pl.when((i >= 1) & (i < ATT))
    def _():
        attend(project)

    @pl.when(i == ATT)
    def _():
        attend(lambda: lambda: None)
        a_ref[...] = acc[...].astype(BF)

    for s in range(8):
        @pl.when(i == D0 + s)
        def _(s=s):
            if s == 1:
                part().wait_recv()
            if s in (3, 5):
                for n in range(CH):
                    fwd((s - 3) // 2, n).wait_recv()
            if s == 6:
                for n in range(CH // 2):
                    for link in range(2):
                        relay(link, n).wait_recv()
                        fwd3(link, n).start()
            if s == 7:
                for n in range(CH // 2):
                    for link in range(2):
                        fwd3(link, n).wait_recv()
            if s:
                met(s).wait_recv()
            e0 = lax.axis_index('ep') * el
            _dispatch(meta[s], u[s], e0.astype(F32), cap, rows, xs.at[s], gt_ref.at[0])

    @pl.when(i >= E0)
    def _():
        e = i - E0
        for j in range(2):
            weights(e, j).wait()
        x = xs[:, pl.ds(pl.multiple_of(e * cap, cap), cap), :].reshape(8 * cap, d)
        h1 = _dot(x, ring[e % RING, 0])
        h3 = _dot(x, ring[e % RING, 1])
        hid_ref[0] = (h1 * jax.nn.sigmoid(h1) * h3).astype(BF)

        @pl.when(e < el - RING)
        def _():
            for j in range(2):
                weights(e + RING, j).start()

    @pl.when(i == E0 + el - 1)
    def _():
        part().wait_send()
        for link in range(2):
            for n in range(CH):
                own(link, n).wait_send()
                fwd(link, n).wait_send()
                if n < CH // 2:
                    relay(link, n).wait_send()
                    fwd3(link, n).wait_send()
        for q in range(1, 8):
            met(q).wait_send()


def _front(h0, idx, slot, na, nm, cos, sin, wr, wq, wk, wv, wo, ue1, ue3, cap):
    t, d = h0.shape
    el, _, fe = ue1.shape
    rows = el * cap
    qb = wq.shape[1] // ATT
    kv = wk.shape[1] // HEAD
    full = lambda a: pl.BlockSpec(a.shape, lambda i: (0,) * a.ndim, pipeline_mode=pl.Buffered(1))
    one = pl.BlockSpec((t, d), lambda i: (0, 0), pipeline_mode=pl.Buffered(1))
    att = lambda i: jnp.minimum(i, ATT - 1)
    prev = lambda i: jnp.clip(i - 1, 0, ATT - 1)
    src = lambda i: jnp.clip(i - D0, 0, 7)
    hbm = pl.BlockSpec(memory_space=pl.ANY)
    dma = pltpu.SemaphoreType.DMA
    return pl.pallas_call(
        lambda *refs: _front_kernel(cap, *refs),
        grid=(E0 + el,),
        in_specs=[full(h0), full(idx), full(slot), full(na), full(nm), full(cos), full(sin), full(wr),
                  pl.BlockSpec((d, qb), lambda i: (0, att(i))),
                  pl.BlockSpec((d, HEAD), lambda i: (0, att(i) * kv // ATT)),
                  pl.BlockSpec((d, HEAD), lambda i: (0, att(i) * kv // ATT)),
                  pl.BlockSpec((qb, d), lambda i: (prev(i), 0)), hbm, hbm],
        out_specs=[pl.BlockSpec((1, 8 * cap, fe), lambda i: (jnp.maximum(i - E0, 0), 0, 0)),
                   pl.BlockSpec((1, 3 * t, rows), lambda i: (src(i), 0, 0)), one],
        out_shape=[jax.ShapeDtypeStruct((el, 8 * cap, fe), BF), jax.ShapeDtypeStruct((8, 3 * t, rows), BF),
                   jax.ShapeDtypeStruct((t, d), BF)],
        scratch_shapes=[pltpu.VMEM((8, t, d), BF), pltpu.VMEM((8, 3 * idx.shape[1], t), F32),
                        pltpu.VMEM((t, d), F32),
                        pltpu.VMEM((2, t, HEAD), BF), pltpu.VMEM((2, t, HEAD), BF),
                        pltpu.VMEM((8, rows, d), BF), pltpu.VMEM((RING, 2, d, fe), BF),
                        dma((2, CH)), dma((2, CH)), dma((1,)), dma((1,)), dma((4, CH)), dma((4, CH)),
                        dma((2, CH)), dma((2, CH)), dma((8,)), dma((8,)), dma((RING, 2))],
        compiler_params=pltpu.CompilerParams(dimension_semantics=('arbitrary',), collective_id=0, has_side_effects=True,
                                             vmem_limit_bytes=67043328),
        name='gather_attention_up',
    )(h0, idx, slot, na, nm, cos, sin, wr, wq, wk, wv, wo, ue1, ue3)


NC = 8
FS = 16
LANES = 128
POS = ((0, 2, 1, 3), (0, 1, 2, 3))


def _down_kernel(cap, hid_ref, gt_ref, a_ref, nf_ref, ue2_ref, w1_ref, w3_ref, w2_ref, out_ref,
                 zb, yb, mo, mp, r0, r1, r2, acc, d_s, d_r, credit, p1_s, p1_r, p2_s, p2_r):
    i = pl.program_id(0)
    peers = _peers()
    el, m, fe = hid_ref.shape
    t = a_ref.shape[0]

    def rc(src, dst, ss, rs, peer):
        return pltpu.make_async_remote_copy(src_ref=src, dst_ref=dst, send_sem=ss, recv_sem=rs,
                                            device_id={'ep': peer}, device_id_type=MESH)

    def pair(c):
        return rc(mo.at[c % 2], r0.at[c % 2], d_s.at[c % 2], d_r.at[c % 2], peers[1])

    def first(c, b):
        return rc(mp.at[c, b, pl.ds(2, 2)], r1.at[c, b], p1_s.at[c, b], p1_r.at[c, b], peers[2 + 2 * b])

    def second(c, b):
        return rc(mp.at[c, b, 1], r2.at[c, b], p2_s.at[c, b], p2_r.at[c, b], peers[4 - 2 * b])

    def second_step(c):
        for b in range(2):
            first(c, b).wait_recv()
            mp[c, b, pl.ds(0, 2)] = mp[c, b, pl.ds(0, 2)] + r1[c, b]
            second(c, b).start()

    def ffn_up():
        z = zb[...]
        h1 = _dot(z, w1_ref[...])
        h3 = _dot(z, w3_ref[...])
        return (h1 * jax.nn.sigmoid(h1) * h3).astype(BF)

    @pl.when(i == 0)
    def _():
        barrier = pltpu.get_barrier_semaphore()
        for s in (1, 2, 4):
            pl.semaphore_signal(barrier, inc=1, device_id={'ep': peers[s]}, device_id_type=MESH)
        acc[...] = a_ref[...].astype(F32)
        zb[...] = _rms_rows(a_ref[...], nf_ref[...])
        pl.semaphore_wait(barrier, 3)

    @pl.when((i >= 1) & (i <= NC))
    def _():
        c = i - 1
        pair(c).wait()
        mp[c] = mp[c] + r0[c % 2]

        @pl.when(c < NC - 2)
        def _():
            pl.semaphore_signal(credit, inc=1, device_id={'ep': peers[1]}, device_id_type=MESH)

        for b in range(2):
            first(c, b).start()

    @pl.when((i >= 2) & (i < NC))
    def _():
        pl.semaphore_wait(credit, 1)

    @pl.when((i >= LAG) & (i < NC))
    def _():
        second_step(i - LAG)

    for c in range(NC - LAG, NC):
        @pl.when(i == NC + 1 + LATE * (c - NC + LAG))
        def _(c=c):
            second_step(c)

    @pl.when(i < NC)
    def _():
        for e in range(el):
            y = _dot(hid_ref[e], ue2_ref[e]).astype(BF)
            for s in range(8):
                yb[s, e * cap:(e + 1) * cap, :] = y[s * cap:(s + 1) * cap]
        hf = ffn_up()
        for s in range(8):
            v = _dot(gt_ref[s], yb[s])
            v = v[:t] + v[t:2 * t] + v[2 * t:]
            for b in range(2):
                dst = v[:, b * LANES:(b + 1) * LANES]
                if s % 2:
                    mo[i % 2, b, POS[b][s // 2]] = dst
                else:
                    mp[i, b, POS[b][s // 2]] = dst
        pair(i).start()
        acc[...] += _dot(hf, w2_ref[...])

    @pl.when(i >= NC)
    def _():
        acc[...] += _dot(ffn_up(), w2_ref[...])

    @pl.when(i == FS - 1)
    def _():
        for c in range(NC):
            for b in range(2):
                second(c, b).wait_recv()
                col = pl.ds((2 * c + b) * LANES, LANES)
                out_ref[:, col] = (acc[:, col] + (mp[c, b, 0] + r2[c, b])).astype(BF)
        for c in range(NC):
            for b in range(2):
                first(c, b).wait_send()
                second(c, b).wait_send()


LAG = 3
LATE = 2


def _down(hid, gt, a, nf, ue2, w1, w3, w2, cap):
    el, m, fe = hid.shape
    t, d = a.shape
    nb = d // NC
    fb = w1.shape[1] // FS
    full = lambda v: pl.BlockSpec(v.shape, lambda i: (0,) * v.ndim, pipeline_mode=pl.Buffered(1))
    dma = pltpu.SemaphoreType.DMA
    return pl.pallas_call(
        lambda *refs: _down_kernel(cap, *refs),
        grid=(FS,),
        in_specs=[full(hid), full(gt), full(a), full(nf),
                  pl.BlockSpec((el, fe, nb), lambda i: (0, 0, jnp.minimum(i, NC - 1))),
                  pl.BlockSpec((d, fb), lambda i: (0, i)),
                  pl.BlockSpec((d, fb), lambda i: (0, i)),
                  pl.BlockSpec((fb, d), lambda i: (i, 0))],
        out_specs=pl.BlockSpec((t, d), lambda i: (0, 0), pipeline_mode=pl.Buffered(1)),
        out_shape=jax.ShapeDtypeStruct((t, d), BF),
        scratch_shapes=[pltpu.VMEM((t, d), BF), pltpu.VMEM((8, el * cap, nb), BF),
                        pltpu.VMEM((2, 2, 4, t, LANES), F32), pltpu.VMEM((NC, 2, 4, t, LANES), F32),
                        pltpu.VMEM((2, 2, 4, t, LANES), F32), pltpu.VMEM((NC, 2, 2, t, LANES), F32),
                        pltpu.VMEM((NC, 2, t, LANES), F32), pltpu.VMEM((t, d), F32),
                        dma((2,)), dma((2,)), pltpu.SemaphoreType.REGULAR,
                        dma((NC, 2)), dma((NC, 2)), dma((NC, 2)), dma((NC, 2))],
        compiler_params=pltpu.CompilerParams(dimension_semantics=('arbitrary',), collective_id=1, has_side_effects=True,
                                             vmem_limit_bytes=67043328),
        name='expert_down_ffn',
    )(hid, gt, a, nf, ue2, w1, w3, w2)


def solution(mesh):
    G = mesh.shape['ep']

    def local(h0, idx, slot, na, wq, wk, wv, wo, nf, w1, w3, w2, nm, wr, ue1, ue3, ue2):
        b, s, d = h0.shape
        k = idx.shape[-1]
        el = ue1.shape[0]
        cap = 2 * s * k // (el * G)
        cos, sin = _tables(s)
        h = h0.reshape(s, d)
        hid, gt, a = _front(h, jnp.swapaxes(idx, 1, 2), jnp.swapaxes(slot, 1, 2), na, nm, cos, sin, wr, wq, wk, wv,
                               wo, ue1, ue3, cap)
        return _down(hid, gt, a, nf, ue2, w1, w3, w2, cap).reshape(b, s, d)

    rows_spec = P(('dp', 'ep'))
    in_specs = (rows_spec,) * 3 + (P(),) * 11 + (P('ep'),) * 3
    return jax.shard_map(local, mesh=mesh, in_specs=in_specs, out_specs=rows_spec, check_vma=False)
```

time: 195 us -> 178 us (0.913)
  Pallas kernels: 186 us -> 175 us
  local copies, waits for them, and re-layouts: 6.16 us -> 2.3 us
  other arithmetic: 2.7 us -> 0 us
    pallas_call x3 -> x2, Pallas kernels: 186 us -> 175 us  [the longest x1 90.9 us: _down(): pl.pallas_call(lambda *refs: _down_kernel(cap, *refs), grid=(FS,), in_spe...]
    reshape x3 -> x0, local copies, waits for them, and re-layouts: 3.86 us -> none  [the longest x1 1.29 us: local(): na.reshape(1, d)]
    concatenate x2 -> x0, other arithmetic: 2.15 us -> none  [the longest x1 1.32 us: local(): ist = jnp.concatenate([idx.reshape(s, k).T, slot.reshape(s, k).T], axis=0)]
where the time goes in v2:
time: 178 us
  Pallas kernels  175 us (98%)
  local copies, waits for them, and re-layouts  2.3 us (1%)
    pallas_call x1, Pallas kernels, _down(): pl.pallas_call(lambda *refs: _down_kernel(cap, *refs), grid=(FS,), in_spe...  90.9 us
    pallas_call x1, Pallas kernels, _front(): pl.pallas_call(lambda *refs: _front_kernel(cap, *refs), grid=(E0 + el,),...  84.3 us

profile of v2, /device:TPU:0, one launch (start us, length us, event | category | flops | bytes accessed | tf_op | source)
XLA Modules:
  0.0 177.6 jit_solution(12687505017793612858)
XLA Ops:
  0.0 84.3 %gather_attention_up.1 = (bf16[16,256,768]{2,1,0:T(8,128)(2,1)}, bf16[8,768,512]{2,1,0:T(8,128)(2,1)}, bf16[256,2048]{1,0:T(8,128)(2,1)}) custom-call(bf16[256,2048]{1,0:T(8,128)(2,1)} %bitcast.5, s32[1,8,256]{2,1,0:T(8,128)} %bitcast.6, s32[1,8,256]{2,1,0:T(8,128)} %bitcast.7, bf16[2048]{0:T(1024)(128)(2,1)} %refs_3_.2, bf16[2048]{0:T(1024)(128)(2,1)} %refs_4_.2, ...), custom_call_target="tpu_custom_call" | custom-call | tf_op jit(solution)/shard_map/gather_attention_up/pallas_call | solution.py:283
  84.3 90.9 %expert_down_ffn.1 = bf16[256,2048]{1,0:T(8,128)(2,1)} custom-call(bf16[16,256,768]{2,1,0:T(8,128)(2,1)} %get-tuple-element.8.refs_0_, bf16[8,768,512]{2,1,0:T(8,128)(2,1)} %get-tuple-element.9.refs_1_, bf16[256,2048]{1,0:T(8,128)(2,1)} %get-tuple-element.10.refs_2_, bf16[2048]{0:T(1024)(128)(2,1)} %refs_3_.3, bf16[16,768,2048]{2,1,0:T(8,128)(2,1)} %refs_4_.3, ...), custom_call_target="tpu_custom_call" | custom-call | tf_op jit(solution)/shard_map/expert_down_ffn/pallas_call | solution.py:427
  175.3 2.3 %copy.21 = bf16[1,256,2048]{2,1,0:T(8,128)(2,1)} copy(bf16[1,256,2048]{2,1,0:T(8,128)(2,1)} %bitcast.4) | data formatting | bytes 2097152

commit v3 on v2

--- a/solution.py
+++ b/solution.py
@@ -83,12 +83,13 @@
 def _front_kernel(cap, h0_ref, ix_ref, sl_ref, na_ref, nm_ref, cos_ref, sin_ref, wr_ref, wq_ref, wk_ref, wv_ref,
                   wo_ref, ue1_ref, ue3_ref, hid_ref, gt_ref, a_ref,
                   u, meta, acc, kb, vb, xs, ring, own_s, own_r, part_s, part_r, fwd_s, fwd_r, rel_s, rel_r,
-                  met_s, met_r, ring_s):
+                  met_s, met_r, ring_s, hid_s):
     i = pl.program_id(0)
     peers = _peers()
     t, d = h0_ref.shape
     rows = xs.shape[1]
     el = rows // cap
+    fe = ue1_ref.shape[2]
     hb = wq_ref.shape[1] // HEAD
     ch = t // CH
     order = (tuple(range(CH)), tuple(range(CH // 2, CH)) + tuple(range(CH // 2)))
@@ -238,22 +239,7 @@
             e0 = lax.axis_index('ep') * el
             _dispatch(meta[s], u[s], e0.astype(F32), cap, rows, xs.at[s], gt_ref.at[0])
 
-    @pl.when(i >= E0)
-    def _():
-        e = i - E0
-        for j in range(2):
-            weights(e, j).wait()
-        x = xs[:, pl.ds(pl.multiple_of(e * cap, cap), cap), :].reshape(8 * cap, d)
-        h1 = _dot(x, ring[e % RING, 0])
-        h3 = _dot(x, ring[e % RING, 1])
-        hid_ref[0] = (h1 * jax.nn.sigmoid(h1) * h3).astype(BF)
-
-        @pl.when(e < el - RING)
-        def _():
-            for j in range(2):
-                weights(e + RING, j).start()
-
-    @pl.when(i == E0 + el - 1)
+    @pl.when(i == E0)
     def _():
         part().wait_send()
         for link in range(2):
@@ -265,6 +251,32 @@
                     fwd3(link, n).wait_send()
         for q in range(1, 8):
             met(q).wait_send()
+
+        def put(n, p):
+            return pltpu.make_async_copy(u.at[n, :, pl.ds(p * d // 2, fe)], hid_ref.at[2 * n + p], hid_s.at[n, p])
+
+        @pl.loop(0, el // 2)
+        def _(n):
+            for p in range(2):
+                e = 2 * n + p
+                for j in range(2):
+                    weights(e, j).wait()
+                x = xs[:, pl.ds(pl.multiple_of(e * cap, cap), cap), :].reshape(8 * cap, d)
+                h1 = _dot(x, ring[e % RING, 0])
+                h3 = _dot(x, ring[e % RING, 1])
+                u[n, :, p * d // 2:p * d // 2 + fe] = (h1 * jax.nn.sigmoid(h1) * h3).astype(BF)
+
+                @pl.when(e < el - RING)
+                def _():
+                    for j in range(2):
+                        weights(e + RING, j).start()
+
+                put(n, p).start()
+
+        @pl.loop(0, el // 2)
+        def _(n):
+            for p in range(2):
+                put(n, p).wait()
 
 
 def _front(h0, idx, slot, na, nm, cos, sin, wr, wq, wk, wv, wo, ue1, ue3, cap):
@@ -282,13 +294,13 @@
     dma = pltpu.SemaphoreType.DMA
     return pl.pallas_call(
         lambda *refs: _front_kernel(cap, *refs),
-        grid=(E0 + el,),
+        grid=(E0 + 1,),
         in_specs=[full(h0), full(idx), full(slot), full(na), full(nm), full(cos), full(sin), full(wr),
                   pl.BlockSpec((d, qb), lambda i: (0, att(i))),
                   pl.BlockSpec((d, HEAD), lambda i: (0, att(i) * kv // ATT)),
                   pl.BlockSpec((d, HEAD), lambda i: (0, att(i) * kv // ATT)),
                   pl.BlockSpec((qb, d), lambda i: (prev(i), 0)), hbm, hbm],
-        out_specs=[pl.BlockSpec((1, 8 * cap, fe), lambda i: (jnp.maximum(i - E0, 0), 0, 0)),
+        out_specs=[hbm,
                    pl.BlockSpec((1, 3 * t, rows), lambda i: (src(i), 0, 0)), one],
         out_shape=[jax.ShapeDtypeStruct((el, 8 * cap, fe), BF), jax.ShapeDtypeStruct((8, 3 * t, rows), BF),
                    jax.ShapeDtypeStruct((t, d), BF)],
@@ -297,7 +309,7 @@
                         pltpu.VMEM((2, t, HEAD), BF), pltpu.VMEM((2, t, HEAD), BF),
                         pltpu.VMEM((8, rows, d), BF), pltpu.VMEM((RING, 2, d, fe), BF),
                         dma((2, CH)), dma((2, CH)), dma((1,)), dma((1,)), dma((4, CH)), dma((4, CH)),
-                        dma((2, CH)), dma((2, CH)), dma((8,)), dma((8,)), dma((RING, 2))],
+                        dma((2, CH)), dma((2, CH)), dma((8,)), dma((8,)), dma((RING, 2)), dma((el // 2, 2))],
         compiler_params=pltpu.CompilerParams(dimension_semantics=('arbitrary',), collective_id=0, has_side_effects=True,
                                              vmem_limit_bytes=67043328),
         name='gather_attention_up',
@@ -305,17 +317,24 @@
 
 
 NC = 8
-FS = 16
+FS = 12
 LANES = 128
+LAG = 2
+LATE = 3
 POS = ((0, 2, 1, 3), (0, 1, 2, 3))
-
-
-def _down_kernel(cap, hid_ref, gt_ref, a_ref, nf_ref, ue2_ref, w1_ref, w3_ref, w2_ref, out_ref,
-                 zb, yb, mo, mp, r0, r1, r2, acc, d_s, d_r, credit, p1_s, p1_r, p2_s, p2_r):
+QE = 2
+
+
+def _down_kernel(cap, nf_ref, hid_ref, gt_ref, a_ref, ue2_ref, w1_ref, w3_ref, w2_ref, out_ref,
+                 hv, gv, ev, w1v, w3v, w2v, hf, yb, mo, mp, r0, r1, r2, acc,
+                 h_s, g_s, a_s, e_s, w_s, d_s, d_r, credit, p1_s, p1_r, p2_s, p2_r):
     i = pl.program_id(0)
     peers = _peers()
     el, m, fe = hid_ref.shape
-    t = a_ref.shape[0]
+    t, d = a_ref.shape
+    nb = d // NC
+    fb = w1v.shape[2]
+    qe = el // QE
 
     def rc(src, dst, ss, rs, peer):
         return pltpu.make_async_remote_copy(src_ref=src, dst_ref=dst, send_sem=ss, recv_sem=rs,
@@ -336,69 +355,126 @@
             mp[c, b, pl.ds(0, 2)] = mp[c, b, pl.ds(0, 2)] + r1[c, b]
             second(c, b).start()
 
-    def ffn_up():
-        z = zb[...]
-        h1 = _dot(z, w1_ref[...])
-        h3 = _dot(z, w3_ref[...])
-        return (h1 * jax.nn.sigmoid(h1) * h3).astype(BF)
+    def load_hid(q):
+        sl = pl.ds(q * qe, qe)
+        return pltpu.make_async_copy(hid_ref.at[sl], hv.at[sl], h_s.at[q])
+
+    def load_gt(q):
+        sl = pl.ds(q * 4, 4)
+        return pltpu.make_async_copy(gt_ref.at[sl], gv.at[sl], g_s.at[q])
+
+    def load_a():
+        return pltpu.make_async_copy(a_ref, out_ref, a_s.at[0])
+
+    def load_down(c, q):
+        sl = pl.ds(q * qe, qe)
+        return pltpu.make_async_copy(ue2_ref.at[sl, :, pl.ds(pl.multiple_of(c * nb, nb), nb)], ev.at[c % 2, sl],
+                                     e_s.at[c % 2, q])
+
+    def load_ffn(n):
+        sl = pl.ds(pl.multiple_of(n * fb, fb), fb)
+        k = n % 2
+        return (pltpu.make_async_copy(w1_ref.at[:, sl], w1v.at[k], w_s.at[k, 0]),
+                pltpu.make_async_copy(w3_ref.at[:, sl], w3v.at[k], w_s.at[k, 1]),
+                pltpu.make_async_copy(w2_ref.at[sl], w2v.at[k], w_s.at[k, 2]))
 
     @pl.when(i == 0)
     def _():
         barrier = pltpu.get_barrier_semaphore()
         for s in (1, 2, 4):
             pl.semaphore_signal(barrier, inc=1, device_id={'ep': peers[s]}, device_id_type=MESH)
-        acc[...] = a_ref[...].astype(F32)
-        zb[...] = _rms_rows(a_ref[...], nf_ref[...])
+        for q in range(QE):
+            load_hid(q).start()
+            load_down(0, q).start()
+        for q in range(2):
+            load_gt(q).start()
+        load_a().start()
+        for cp in load_ffn(0):
+            cp.start()
+        for q in range(QE):
+            load_hid(q).wait()
         pl.semaphore_wait(barrier, 3)
 
-    @pl.when((i >= 1) & (i <= NC))
-    def _():
-        c = i - 1
-        pair(c).wait()
-        mp[c] = mp[c] + r0[c % 2]
-
-        @pl.when(c < NC - 2)
+    @pl.when(i + 1 < NC)
+    def _():
+        for q in range(QE):
+            load_down(i + 1, q).start()
+
+    @pl.when(i + 1 < FS)
+    def _():
+        for cp in load_ffn(i + 1):
+            cp.start()
+
+    @pl.when((i >= LAG) & (i < NC))
+    def _():
+        second_step(i - LAG)
+
+    for c in range(NC - LAG, NC):
+        @pl.when(i == NC + LATE * (c - NC + LAG))
+        def _(c=c):
+            second_step(c)
+
+    @pl.when(i < NC)
+    def _():
+        for q in range(QE):
+            load_down(i, q).wait()
+            for e in range(q * qe, (q + 1) * qe):
+                y = _dot(hv[e], ev[i % 2, e]).astype(BF)
+                for s in range(8):
+                    yb[s, e * cap:(e + 1) * cap, :] = y[s * cap:(s + 1) * cap]
+
+    @pl.when(i == 0)
+    def _():
+        for q in range(2):
+            load_gt(q).wait()
+
+    @pl.when((i >= 2) & (i < NC))
+    def _():
+        pl.semaphore_wait(credit, 1)
+
+    def combine(s):
+        v = _dot(gv[s], yb[s])
+        v = v[:t] + v[t:2 * t] + v[2 * t:]
+        for b in range(2):
+            dst = v[:, b * LANES:(b + 1) * LANES]
+            if s % 2:
+                mo[i % 2, b, POS[b][s // 2]] = dst
+            else:
+                mp[i, b, POS[b][s // 2]] = dst
+
+    @pl.when(i < NC)
+    def _():
+        for s in range(1, 8, 2):
+            combine(s)
+        pair(i).start()
+        for s in range(0, 8, 2):
+            combine(s)
+
+    @pl.when(i == 0)
+    def _():
+        load_a().wait()
+        acc[...] = out_ref[...].astype(F32)
+        out_ref[...] = _rms_rows(out_ref[...], nf_ref[...])
+
+    for cp in load_ffn(i):
+        cp.wait()
+    h1 = _dot(out_ref[...], w1v[i % 2])
+    h3 = _dot(out_ref[...], w3v[i % 2])
+    hf[...] = (h1 * jax.nn.sigmoid(h1) * h3).astype(BF)
+
+    @pl.when(i < NC)
+    def _():
+        pair(i).wait()
+        mp[i] = mp[i] + r0[i % 2]
+
+        @pl.when(i < NC - 2)
         def _():
             pl.semaphore_signal(credit, inc=1, device_id={'ep': peers[1]}, device_id_type=MESH)
 
         for b in range(2):
-            first(c, b).start()
-
-    @pl.when((i >= 2) & (i < NC))
-    def _():
-        pl.semaphore_wait(credit, 1)
-
-    @pl.when((i >= LAG) & (i < NC))
-    def _():
-        second_step(i - LAG)
-
-    for c in range(NC - LAG, NC):
-        @pl.when(i == NC + 1 + LATE * (c - NC + LAG))
-        def _(c=c):
-            second_step(c)
-
-    @pl.when(i < NC)
-    def _():
-        for e in range(el):
-            y = _dot(hid_ref[e], ue2_ref[e]).astype(BF)
-            for s in range(8):
-                yb[s, e * cap:(e + 1) * cap, :] = y[s * cap:(s + 1) * cap]
-        hf = ffn_up()
-        for s in range(8):
-            v = _dot(gt_ref[s], yb[s])
-            v = v[:t] + v[t:2 * t] + v[2 * t:]
-            for b in range(2):
-                dst = v[:, b * LANES:(b + 1) * LANES]
-                if s % 2:
-                    mo[i % 2, b, POS[b][s // 2]] = dst
-                else:
-                    mp[i, b, POS[b][s // 2]] = dst
-        pair(i).start()
-        acc[...] += _dot(hf, w2_ref[...])
-
-    @pl.when(i >= NC)
-    def _():
-        acc[...] += _dot(ffn_up(), w2_ref[...])
+            first(i, b).start()
+
+    acc[...] += _dot(hf[...], w2v[i % 2])
 
     @pl.when(i == FS - 1)
     def _():
@@ -413,37 +489,33 @@
                 second(c, b).wait_send()
 
 
-LAG = 3
-LATE = 2
-
-
 def _down(hid, gt, a, nf, ue2, w1, w3, w2, cap):
     el, m, fe = hid.shape
     t, d = a.shape
     nb = d // NC
     fb = w1.shape[1] // FS
-    full = lambda v: pl.BlockSpec(v.shape, lambda i: (0,) * v.ndim, pipeline_mode=pl.Buffered(1))
+    hbm = pl.BlockSpec(memory_space=pl.ANY)
     dma = pltpu.SemaphoreType.DMA
     return pl.pallas_call(
         lambda *refs: _down_kernel(cap, *refs),
         grid=(FS,),
-        in_specs=[full(hid), full(gt), full(a), full(nf),
-                  pl.BlockSpec((el, fe, nb), lambda i: (0, 0, jnp.minimum(i, NC - 1))),
-                  pl.BlockSpec((d, fb), lambda i: (0, i)),
-                  pl.BlockSpec((d, fb), lambda i: (0, i)),
-                  pl.BlockSpec((fb, d), lambda i: (i, 0))],
+        in_specs=[pl.BlockSpec(nf.shape, lambda i: (0,), pipeline_mode=pl.Buffered(1))] + [hbm] * 7,
         out_specs=pl.BlockSpec((t, d), lambda i: (0, 0), pipeline_mode=pl.Buffered(1)),
         out_shape=jax.ShapeDtypeStruct((t, d), BF),
-        scratch_shapes=[pltpu.VMEM((t, d), BF), pltpu.VMEM((8, el * cap, nb), BF),
+        scratch_shapes=[pltpu.VMEM(hid.shape, BF), pltpu.VMEM(gt.shape, BF),
+                        pltpu.VMEM((2, el, fe, nb), BF), pltpu.VMEM((2, d, fb), BF), pltpu.VMEM((2, d, fb), BF),
+                        pltpu.VMEM((2, fb, d), BF), pltpu.VMEM((t, fb), BF),
+                        pltpu.VMEM((8, el * cap, nb), BF),
                         pltpu.VMEM((2, 2, 4, t, LANES), F32), pltpu.VMEM((NC, 2, 4, t, LANES), F32),
                         pltpu.VMEM((2, 2, 4, t, LANES), F32), pltpu.VMEM((NC, 2, 2, t, LANES), F32),
                         pltpu.VMEM((NC, 2, t, LANES), F32), pltpu.VMEM((t, d), F32),
+                        dma((QE,)), dma((2,)), dma((1,)), dma((2, QE)), dma((2, 3)),
                         dma((2,)), dma((2,)), pltpu.SemaphoreType.REGULAR,
                         dma((NC, 2)), dma((NC, 2)), dma((NC, 2)), dma((NC, 2))],
         compiler_params=pltpu.CompilerParams(dimension_semantics=('arbitrary',), collective_id=1, has_side_effects=True,
                                              vmem_limit_bytes=67043328),
         name='expert_down_ffn',
-    )(hid, gt, a, nf, ue2, w1, w3, w2)
+    )(nf, hid, gt, a, ue2, w1, w3, w2)
 
 
 def solution(mesh):

time: 178 us -> 169 us (0.949)
  Pallas kernels: 175 us -> 166 us
    pallas_call x1, Pallas kernels: 90.9 us -> 85.1 us  [_down(): pl.pallas_call(lambda *refs: _down_kernel(cap, *refs), grid=(FS,), in_spe...]
    pallas_call x1, Pallas kernels: 84.3 us -> 81.2 us  [_front(): pl.pallas_call(lambda *refs: _front_kernel(cap, *refs), grid=(E0 + 1,), i...]
where the time goes in v3:
time: 169 us
  Pallas kernels  166 us (98%)
  local copies, waits for them, and re-layouts  2.3 us (1%)
    pallas_call x1, Pallas kernels, _down(): pl.pallas_call(lambda *refs: _down_kernel(cap, *refs), grid=(FS,), in_spe...  85.1 us
    pallas_call x1, Pallas kernels, _front(): pl.pallas_call(lambda *refs: _front_kernel(cap, *refs), grid=(E0 + 1,), i...  81.2 us

profile of v3, /device:TPU:0, one launch (start us, length us, event | category | flops | bytes accessed | tf_op | source)
XLA Modules:
  0.0 168.5 jit_solution(2952117790436060926)
XLA Ops:
  0.0 81.2 %gather_attention_up.1 = (bf16[16,256,768]{2,1,0:T(8,128)(2,1)}, bf16[8,768,512]{2,1,0:T(8,128)(2,1)}, bf16[256,2048]{1,0:T(8,128)(2,1)}) custom-call(bf16[256,2048]{1,0:T(8,128)(2,1)} %bitcast.5, s32[1,8,256]{2,1,0:T(8,128)} %bitcast.6, s32[1,8,256]{2,1,0:T(8,128)} %bitcast.7, bf16[2048]{0:T(1024)(128)(2,1)} %refs_3_.1, bf16[2048]{0:T(1024)(128)(2,1)} %refs_4_.2, ...), custom_call_target="tpu_custom_call" | custom-call | tf_op jit(solution)/shard_map/gather_attention_up/pallas_call | solution.py:295
  81.2 85.1 %expert_down_ffn.1 = bf16[256,2048]{1,0:T(8,128)(2,1)} custom-call(bf16[2048]{0:T(1024)(128)(2,1)} %refs_0_.1, bf16[16,256,768]{2,1,0:T(8,128)(2,1)} %get-tuple-element.8.refs_1_, bf16[8,768,512]{2,1,0:T(8,128)(2,1)} %get-tuple-element.9.refs_2_, bf16[256,2048]{1,0:T(8,128)(2,1)} %get-tuple-element.10.refs_3_, bf16[16,768,2048]{2,1,0:T(8,128)(2,1)} %refs_4_.3, ...), custom_call_target="tpu_custom_call" | custom-call | tf_op jit(solution)/shard_map/expert_down_ffn/pallas_call | solution.py:499
  166.2 2.3 %copy.21 = bf16[1,256,2048]{2,1,0:T(8,128)(2,1)} copy(bf16[1,256,2048]{2,1,0:T(8,128)(2,1)} %bitcast.4) | data formatting | bytes 2097152

commit v4 on v3

--- a/solution.py
+++ b/solution.py
@@ -45,7 +45,7 @@
     return (xf * r * w.astype(F32)).astype(BF)
 
 
-def _dispatch(meta, u, e0, cap, rows, x_ref, gt_ref):
+def _places(meta, e0, cap, rows, d_ref, gt_ref):
     k = meta.shape[0] // 3
     t = meta.shape[1]
     idx, slot, g = meta[:k], meta[k:2 * k], meta[2 * k:3 * k]
@@ -61,6 +61,7 @@
             d = jnp.where(hit, 1.0, d)
             gt = jnp.where(hit, g[j:j + 1, :], gt)
         col = pl.ds(b * step, step)
+        d_ref[col, :] = d.astype(BF)
         gt = gt.T
         hi = gt.astype(BF)
         rest = gt - hi.astype(F32)
@@ -69,7 +70,6 @@
         gt_ref[0:t, col] = hi
         gt_ref[t:2 * t, col] = mid
         gt_ref[2 * t:3 * t, col] = lo
-        x_ref[pl.ds(b * step, step), :] = _dot(d.astype(BF), u).astype(BF)
 
 
 ATT = 8
@@ -82,15 +82,16 @@
 
 def _front_kernel(cap, h0_ref, ix_ref, sl_ref, na_ref, nm_ref, cos_ref, sin_ref, wr_ref, wq_ref, wk_ref, wv_ref,
                   wo_ref, ue1_ref, ue3_ref, hid_ref, gt_ref, a_ref,
-                  u, meta, acc, kb, vb, xs, ring, own_s, own_r, part_s, part_r, fwd_s, fwd_r, rel_s, rel_r,
-                  met_s, met_r, ring_s, hid_s):
+                  u, meta, acc, kb, vb, xs, ring, db, wqv, wkv, wvv, wov, wrv, own_s, own_r, part_s, part_r, fwd_s, fwd_r, rel_s, rel_r,
+                  met_s, met_r, ring_s, hid_s, q_s, kv_s, o_s, wr_s):
     i = pl.program_id(0)
     peers = _peers()
     t, d = h0_ref.shape
     rows = xs.shape[1]
     el = rows // cap
     fe = ue1_ref.shape[2]
-    hb = wq_ref.shape[1] // HEAD
+    qw = wqv.shape[2]
+    hb = qw // HEAD
     ch = t // CH
     order = (tuple(range(CH)), tuple(range(CH // 2, CH)) + tuple(range(CH // 2)))
 
@@ -122,6 +123,21 @@
 
     def weights(e, j):
         return pltpu.make_async_copy((ue1_ref, ue3_ref)[j].at[e], ring.at[e % RING, j], ring_s.at[e % RING, j])
+
+    def load_q(n):
+        sl = pl.ds(pl.multiple_of(n * qw, qw), qw)
+        return pltpu.make_async_copy(wq_ref.at[:, sl], wqv.at[n % 2], q_s.at[n % 2])
+
+    def load_o(n):
+        sl = pl.ds(pl.multiple_of(n * qw, qw), qw)
+        return pltpu.make_async_copy(wo_ref.at[sl], wov.at[n % 2], o_s.at[n % 2])
+
+    def load_kv(g, j):
+        sl = pl.ds(pl.multiple_of(g * HEAD, HEAD), HEAD)
+        return pltpu.make_async_copy((wk_ref, wv_ref)[j].at[:, sl], (wkv, wvv)[j].at[g % 2], kv_s.at[g % 2, j])
+
+    def load_r():
+        return pltpu.make_async_copy(wr_ref, wrv, wr_s.at[0])
 
     def pass_on(n):
         for link in range(2):
@@ -142,12 +158,14 @@
             for link in range(2):
                 own(link, n).start()
         part().start()
-        for e in range(RING):
-            for j in range(2):
-                weights(e, j).start()
+        load_r().start()
+        load_q(0).start()
+        for j in range(2):
+            load_kv(0, j).start()
         xs[7, 0:t] = _rms_rows(h0_ref[...], na_ref[...])
         k = ix_ref.shape[1]
-        lt = _dot(uu, wr_ref[...]).T
+        load_r().wait()
+        lt = _dot(uu, wrv[...]).T
         it = ix_ref[0]
         ids = lax.broadcasted_iota(jnp.int32, lt.shape, 0)
         sel = [jnp.sum(jnp.where(ids == it[j:j + 1, :], lt, 0.0), axis=0, keepdims=True) for j in range(k)]
@@ -163,6 +181,25 @@
         for s in range(1, 8):
             met(s).start()
 
+    @pl.when(i == ATT // 2)
+    def _():
+        for e in range(RING):
+            for j in range(2):
+                weights(e, j).start()
+
+    @pl.when(i + 1 < ATT)
+    def _():
+        load_q(i + 1).start()
+
+    @pl.when(i < ATT)
+    def _():
+        load_o(i).start()
+
+    @pl.when((i % 2 == 1) & (i + 1 < ATT))
+    def _():
+        for j in range(2):
+            load_kv((i + 1) // 2, j).start()
+
     for n in range(CH):
         @pl.when(i == PASS[n])
         def _(n=n):
@@ -172,7 +209,7 @@
         return (v * cos_ref[...] + pltpu.roll(v, HEAD // 2, 1) * sin_ref[...]).astype(BF)
 
     def project():
-        q = _dot(xs[7, 0:t], wq_ref[...])
+        q = _dot(xs[7, 0:t], wqv[i % 2])
 
         def finish():
             for h in range(hb):
@@ -181,8 +218,10 @@
 
     def keys():
         g = (i // 2) % 2
-        kb[g] = rope(_dot(xs[7, 0:t], wk_ref[...]))
-        vb[g] = _dot(xs[7, 0:t], wv_ref[...]).astype(BF)
+        for j in range(2):
+            load_kv(i // 2, j).wait()
+        kb[g] = rope(_dot(xs[7, 0:t], wkv[g]))
+        vb[g] = _dot(xs[7, 0:t], wvv[g]).astype(BF)
 
     def attend(between):
         g = ((i - 1) // 2) % 2
@@ -198,11 +237,19 @@
             p = (ex / jnp.sum(ex, axis=1, keepdims=True)).astype(BF)
             o.append(_dot(p, vv).astype(BF))
         finish()
-        acc[...] += _dot(jnp.concatenate(o, axis=1), wo_ref[...])
+        acc[...] += _dot(jnp.concatenate(o, axis=1), wov[(i - 1) % 2])
 
     @pl.when((i < ATT) & (i % 2 == 0))
     def _():
         keys()
+
+    @pl.when(i < ATT)
+    def _():
+        load_q(i).wait()
+
+    @pl.when((i >= 1) & (i <= ATT))
+    def _():
+        load_o(i - 1).wait()
 
     @pl.when(i == 0)
     def _():
@@ -220,6 +267,10 @@
     for s in range(8):
         @pl.when(i == D0 + s)
         def _(s=s):
+            if s:
+                met(s).wait_recv()
+            e0 = lax.axis_index('ep') * el
+            _places(meta[s], e0.astype(F32), cap, rows, db, gt_ref.at[0])
             if s == 1:
                 part().wait_recv()
             if s in (3, 5):
@@ -234,10 +285,7 @@
                 for n in range(CH // 2):
                     for link in range(2):
                         fwd3(link, n).wait_recv()
-            if s:
-                met(s).wait_recv()
-            e0 = lax.axis_index('ep') * el
-            _dispatch(meta[s], u[s], e0.astype(F32), cap, rows, xs.at[s], gt_ref.at[0])
+            xs[s] = _dot(db[...], u[s]).astype(BF)
 
     @pl.when(i == E0)
     def _():
@@ -284,22 +332,19 @@
     el, _, fe = ue1.shape
     rows = el * cap
     qb = wq.shape[1] // ATT
-    kv = wk.shape[1] // HEAD
     full = lambda a: pl.BlockSpec(a.shape, lambda i: (0,) * a.ndim, pipeline_mode=pl.Buffered(1))
     one = pl.BlockSpec((t, d), lambda i: (0, 0), pipeline_mode=pl.Buffered(1))
-    att = lambda i: jnp.minimum(i, ATT - 1)
-    prev = lambda i: jnp.clip(i - 1, 0, ATT - 1)
-    src = lambda i: jnp.clip(i - D0, 0, 7)
+
+    def src(i):
+        s = jnp.clip(i - D0, 0, 7)
+        return s // 2 + 4 * (1 - s % 2)
+
     hbm = pl.BlockSpec(memory_space=pl.ANY)
     dma = pltpu.SemaphoreType.DMA
     return pl.pallas_call(
         lambda *refs: _front_kernel(cap, *refs),
         grid=(E0 + 1,),
-        in_specs=[full(h0), full(idx), full(slot), full(na), full(nm), full(cos), full(sin), full(wr),
-                  pl.BlockSpec((d, qb), lambda i: (0, att(i))),
-                  pl.BlockSpec((d, HEAD), lambda i: (0, att(i) * kv // ATT)),
-                  pl.BlockSpec((d, HEAD), lambda i: (0, att(i) * kv // ATT)),
-                  pl.BlockSpec((qb, d), lambda i: (prev(i), 0)), hbm, hbm],
+        in_specs=[full(h0), full(idx), full(slot), full(na), full(nm), full(cos), full(sin)] + [hbm] * 7,
         out_specs=[hbm,
                    pl.BlockSpec((1, 3 * t, rows), lambda i: (src(i), 0, 0)), one],
         out_shape=[jax.ShapeDtypeStruct((el, 8 * cap, fe), BF), jax.ShapeDtypeStruct((8, 3 * t, rows), BF),
@@ -308,8 +353,11 @@
                         pltpu.VMEM((t, d), F32),
                         pltpu.VMEM((2, t, HEAD), BF), pltpu.VMEM((2, t, HEAD), BF),
                         pltpu.VMEM((8, rows, d), BF), pltpu.VMEM((RING, 2, d, fe), BF),
+                        pltpu.VMEM((rows, t), BF), pltpu.VMEM((2, d, qb), BF), pltpu.VMEM((2, d, HEAD), BF),
+                        pltpu.VMEM((2, d, HEAD), BF), pltpu.VMEM((2, qb, d), BF), pltpu.VMEM(wr.shape, BF),
                         dma((2, CH)), dma((2, CH)), dma((1,)), dma((1,)), dma((4, CH)), dma((4, CH)),
-                        dma((2, CH)), dma((2, CH)), dma((8,)), dma((8,)), dma((RING, 2)), dma((el // 2, 2))],
+                        dma((2, CH)), dma((2, CH)), dma((8,)), dma((8,)), dma((RING, 2)), dma((el // 2, 2)),
+                        dma((2,)), dma((2, 2)), dma((2,)), dma((1,))],
         compiler_params=pltpu.CompilerParams(dimension_semantics=('arbitrary',), collective_id=0, has_side_effects=True,
                                              vmem_limit_bytes=67043328),
         name='gather_attention_up',
@@ -389,21 +437,22 @@
         for q in range(2):
             load_gt(q).start()
         load_a().start()
-        for cp in load_ffn(0):
-            cp.start()
-        for q in range(QE):
-            load_hid(q).wait()
         pl.semaphore_wait(barrier, 3)
 
-    @pl.when(i + 1 < NC)
-    def _():
-        for q in range(QE):
-            load_down(i + 1, q).start()
-
-    @pl.when(i + 1 < FS)
-    def _():
-        for cp in load_ffn(i + 1):
-            cp.start()
+    def prefetch():
+        @pl.when(i + 1 < NC)
+        def _():
+            for q in range(QE):
+                load_down(i + 1, q).start()
+
+        @pl.when(i + 1 < FS)
+        def _():
+            for cp in load_ffn(i + 1):
+                cp.start()
+
+    @pl.when(i > 0)
+    def _():
+        prefetch()
 
     @pl.when((i >= LAG) & (i < NC))
     def _():
@@ -417,6 +466,10 @@
     @pl.when(i < NC)
     def _():
         for q in range(QE):
+            @pl.when(i == 0)
+            def _(q=q):
+                load_hid(q).wait()
+
             load_down(i, q).wait()
             for e in range(q * qe, (q + 1) * qe):
                 y = _dot(hv[e], ev[i % 2, e]).astype(BF)
@@ -425,15 +478,17 @@
 
     @pl.when(i == 0)
     def _():
-        for q in range(2):
-            load_gt(q).wait()
+        load_gt(0).wait()
+        for cp in load_ffn(0):
+            cp.start()
+        prefetch()
 
     @pl.when((i >= 2) & (i < NC))
     def _():
         pl.semaphore_wait(credit, 1)
 
     def combine(s):
-        v = _dot(gv[s], yb[s])
+        v = _dot(gv[s // 2 + 4 * (1 - s % 2)], yb[s])
         v = v[:t] + v[t:2 * t] + v[2 * t:]
         for b in range(2):
             dst = v[:, b * LANES:(b + 1) * LANES]
@@ -447,6 +502,11 @@
         for s in range(1, 8, 2):
             combine(s)
         pair(i).start()
+
+        @pl.when(i == 0)
+        def _():
+            load_gt(1).wait()
+
         for s in range(0, 8, 2):
             combine(s)
 

time: 169 us -> 165 us (0.976)
  Pallas kernels: 166 us -> 163 us
    pallas_call x1, Pallas kernels: 81.2 us -> 78.6 us  [_front(): pl.pallas_call(lambda *refs: _front_kernel(cap, *refs), grid=(E0 + 1,), i...]
where the time goes in v4:
time: 165 us
  Pallas kernels  163 us (99%)
  local copies, waits for them, and re-layouts  2.3 us (1%)
    pallas_call x1, Pallas kernels, _down(): pl.pallas_call(lambda *refs: _down_kernel(cap, *refs), grid=(FS,), in_spe...  84 us
    pallas_call x1, Pallas kernels, _front(): pl.pallas_call(lambda *refs: _front_kernel(cap, *refs), grid=(E0 + 1,), i...  78.6 us

profile of v4, /device:TPU:0, one launch (start us, length us, event | category | flops | bytes accessed | tf_op | source)
XLA Modules:
  0.0 164.9 jit_solution(8659923487023183421)
XLA Ops:
  0.0 78.6 %gather_attention_up.1 = (bf16[16,256,768]{2,1,0:T(8,128)(2,1)}, bf16[8,768,512]{2,1,0:T(8,128)(2,1)}, bf16[256,2048]{1,0:T(8,128)(2,1)}) custom-call(bf16[256,2048]{1,0:T(8,128)(2,1)} %bitcast.5, s32[1,8,256]{2,1,0:T(8,128)} %bitcast.6, s32[1,8,256]{2,1,0:T(8,128)} %bitcast.7, bf16[2048]{0:T(1024)(128)(2,1)} %refs_3_.1, bf16[2048]{0:T(1024)(128)(2,1)} %refs_4_.2, ...), custom_call_target="tpu_custom_call" | custom-call | tf_op jit(solution)/shard_map/gather_attention_up/pallas_call | solution.py:344
  78.6 84.0 %expert_down_ffn.1 = bf16[256,2048]{1,0:T(8,128)(2,1)} custom-call(bf16[2048]{0:T(1024)(128)(2,1)} %refs_0_.1, bf16[16,256,768]{2,1,0:T(8,128)(2,1)} %get-tuple-element.8.refs_1_, bf16[8,768,512]{2,1,0:T(8,128)(2,1)} %get-tuple-element.9.refs_2_, bf16[256,2048]{1,0:T(8,128)(2,1)} %get-tuple-element.10.refs_3_, bf16[16,768,2048]{2,1,0:T(8,128)(2,1)} %refs_4_.3, ...), custom_call_target="tpu_custom_call" | custom-call | tf_op jit(solution)/shard_map/expert_down_ffn/pallas_call | solution.py:559
  162.6 2.3 %copy.21 = bf16[1,256,2048]{2,1,0:T(8,128)(2,1)} copy(bf16[1,256,2048]{2,1,0:T(8,128)(2,1)} %bitcast.4) | data formatting | bytes 2097152

commit v5 on v4

--- a/solution.py
+++ b/solution.py
@@ -516,23 +516,30 @@
         acc[...] = out_ref[...].astype(F32)
         out_ref[...] = _rms_rows(out_ref[...], nf_ref[...])
 
+    def exchange():
+        pair(i).wait()
+        mp[i] = mp[i] + r0[i % 2]
+
+        @pl.when(i < NC - 2)
+        def _():
+            pl.semaphore_signal(credit, inc=1, device_id={'ep': peers[1]}, device_id_type=MESH)
+
+        for b in range(2):
+            first(i, b).start()
+
+    @pl.when(i == 0)
+    def _():
+        exchange()
+
     for cp in load_ffn(i):
         cp.wait()
     h1 = _dot(out_ref[...], w1v[i % 2])
     h3 = _dot(out_ref[...], w3v[i % 2])
     hf[...] = (h1 * jax.nn.sigmoid(h1) * h3).astype(BF)
 
-    @pl.when(i < NC)
-    def _():
-        pair(i).wait()
-        mp[i] = mp[i] + r0[i % 2]
-
-        @pl.when(i < NC - 2)
-        def _():
-            pl.semaphore_signal(credit, inc=1, device_id={'ep': peers[1]}, device_id_type=MESH)
-
-        for b in range(2):
-            first(i, b).start()
+    @pl.when((i > 0) & (i < NC))
+    def _():
+        exchange()
 
     acc[...] += _dot(hf[...], w2v[i % 2])
 

time: 165 us -> 166 us (level)
  no operation moved by 1% of the time
where the time goes in v5:
time: 166 us; the launch traced here: 165 us
  Pallas kernels  163 us (98%)
  local copies, waits for them, and re-layouts  2.3 us (1%)
    pallas_call x1, Pallas kernels, _down(): pl.pallas_call(lambda *refs: _down_kernel(cap, *refs), grid=(FS,), in_spe...  84.5 us
    pallas_call x1, Pallas kernels, _front(): pl.pallas_call(lambda *refs: _front_kernel(cap, *refs), grid=(E0 + 1,), i...  78.6 us

profile of v5, /device:TPU:0, one launch (start us, length us, event | category | flops | bytes accessed | tf_op | source)
XLA Modules:
  0.0 165.4 jit_solution(11642325090811510773)
XLA Ops:
  0.0 78.6 %gather_attention_up.1 = (bf16[16,256,768]{2,1,0:T(8,128)(2,1)}, bf16[8,768,512]{2,1,0:T(8,128)(2,1)}, bf16[256,2048]{1,0:T(8,128)(2,1)}) custom-call(bf16[256,2048]{1,0:T(8,128)(2,1)} %bitcast.5, s32[1,8,256]{2,1,0:T(8,128)} %bitcast.6, s32[1,8,256]{2,1,0:T(8,128)} %bitcast.7, bf16[2048]{0:T(1024)(128)(2,1)} %refs_3_.1, bf16[2048]{0:T(1024)(128)(2,1)} %refs_4_.2, ...), custom_call_target="tpu_custom_call" | custom-call | tf_op jit(solution)/shard_map/gather_attention_up/pallas_call | solution.py:344
  78.6 84.5 %expert_down_ffn.1 = bf16[256,2048]{1,0:T(8,128)(2,1)} custom-call(bf16[2048]{0:T(1024)(128)(2,1)} %refs_0_.1, bf16[16,256,768]{2,1,0:T(8,128)(2,1)} %get-tuple-element.8.refs_1_, bf16[8,768,512]{2,1,0:T(8,128)(2,1)} %get-tuple-element.9.refs_2_, bf16[256,2048]{1,0:T(8,128)(2,1)} %get-tuple-element.10.refs_3_, bf16[16,768,2048]{2,1,0:T(8,128)(2,1)} %refs_4_.3, ...), custom_call_target="tpu_custom_call" | custom-call | tf_op jit(solution)/shard_map/expert_down_ffn/pallas_call | solution.py:566
  163.1 2.3 %copy.21 = bf16[1,256,2048]{2,1,0:T(8,128)(2,1)} copy(bf16[1,256,2048]{2,1,0:T(8,128)(2,1)} %bitcast.4) | data formatting | bytes 2097152
